TPU v7x, 32 devices: a whole 2x2x4 slice. The times are simulated.
32 devices in a mesh: inst: 2 (over x), dev: 4 (over z), side: 4 (over y, core).
Axes of the slice: x: 2, y: 2, z: 4, core: 2. Of those that a mesh axis runs over, the one named last changes fastest.
Arguments:
- hidden: bfloat16 [2048, 4096], P(('inst', 'dev')), parts along dimension 0
- cache_len: int32 [2048], P(('inst', 'dev')), parts along dimension 0
- k_cache: bfloat16 [1, 2048, 8, 64, 128], P(None, ('inst', 'dev')), parts along dimension 1
- v_cache: bfloat16 [1, 2048, 8, 64, 128], P(None, ('inst', 'dev')), parts along dimension 1
- w_q: bfloat16 [1, 4096, 4096], replicated
- w_kv: bfloat16 [1, 4096, 2048], replicated
- w_o: bfloat16 [1, 4096, 4096], replicated
- attn_gain: float32 [1, 4096], replicated
- ffn_gain: float32 [1, 4096], replicated
- w_gate: bfloat16 [1, 4096, 14336], P(None, None, 'dev')
- w_up: bfloat16 [1, 4096, 14336], P(None, None, 'dev')
- w_down: bfloat16 [1, 14336, 4096], P(None, 'dev')
Outputs:
- output: bfloat16 [2048, 4096], P(('inst', 'dev', 'side')), parts along dimension 0
There are 2 independent parts. A program takes and returns all parts, laid end to end along the dimension named above; an argument that names none is the same for every part.
All inputs are finite; a program needn't handle non-finite values.
Results may differ from a plain program's by a relative error of at most 0.0123253.
Values are sent between devices in bfloat16 or wider.
A program may use at most 1 GiB of HBM per device.

v0:
```python
import jax
import jax.numpy as jnp
from jax import lax
from jax.sharding import PartitionSpec as P

EPS = 1e-5
ROPE_BASE = 10000.0


def rms_norm(rows, gain):
    rows_f = rows.astype(jnp.float32)
    inv_rms = lax.rsqrt(jnp.mean(rows_f * rows_f, axis=-1, keepdims=True) + EPS)
    return (rows_f * inv_rms * gain).astype(jnp.bfloat16)


def rotary(vecs, positions):
    half_dim = vecs.shape[-1] // 2
    freqs = ROPE_BASE ** (-jnp.arange(half_dim, dtype=jnp.float32) / half_dim)
    angle = positions.astype(jnp.float32)[:, None, None] * freqs
    cos_part = jnp.cos(angle)
    sin_part = jnp.sin(angle)
    first = vecs[..., :half_dim]
    second = vecs[..., half_dim:]
    return jnp.concatenate([first * cos_part - second * sin_part, second * cos_part + first * sin_part], axis=-1)


def attention_layer(x_rows, lengths, k_seq, v_seq, q_weight, kv_weight, o_weight, gain_attn):
    count = x_rows.shape[0]
    kv_heads = k_seq.shape[1]
    head_dim = k_seq.shape[-1]
    normed = rms_norm(x_rows, gain_attn)
    q_all = jnp.dot(normed, q_weight, preferred_element_type=jnp.float32).reshape(count, -1, head_dim)
    kv_all = jnp.dot(normed, kv_weight, preferred_element_type=jnp.float32).reshape(count, 2, kv_heads, head_dim)
    q_rows = rotary(q_all, lengths).astype(jnp.bfloat16).reshape(count, kv_heads, -1, head_dim)
    k_new = rotary(kv_all[:, 0], lengths).astype(jnp.bfloat16)
    v_new = kv_all[:, 1].astype(jnp.bfloat16)
    scale = head_dim ** -0.5
    scores = jnp.einsum('nkgd,nksd->nkgs', q_rows, k_seq, preferred_element_type=jnp.float32) * scale
    valid = jnp.arange(k_seq.shape[2])[None, None, None, :] < lengths[:, None, None, None]
    scores = jnp.where(valid, scores, -1e30)
    self_score = jnp.einsum('nkgd,nkd->nkg', q_rows, k_new, preferred_element_type=jnp.float32) * scale
    row_max = jnp.maximum(jnp.max(scores, axis=-1), self_score)
    exp_scores = jnp.exp(scores - row_max[..., None])
    self_exp = jnp.exp(self_score - row_max)
    total_exp = jnp.sum(exp_scores, axis=-1) + self_exp
    mixed = jnp.einsum('nkgs,nksd->nkgd', exp_scores.astype(jnp.bfloat16), v_seq, preferred_element_type=jnp.float32)
    mixed = mixed + self_exp.astype(jnp.bfloat16).astype(jnp.float32)[..., None] * v_new.astype(jnp.float32)[:, :, None, :]
    mixed = (mixed / total_exp[..., None]).astype(jnp.bfloat16).reshape(count, -1)
    attn_out = jnp.dot(mixed, o_weight, preferred_element_type=jnp.float32)
    return (x_rows.astype(jnp.float32) + attn_out).astype(jnp.bfloat16)


def ffn_partial(h_rows, gate_weight, up_weight, down_weight):
    gate = jnp.dot(h_rows, gate_weight, preferred_element_type=jnp.float32)
    up_proj = jnp.dot(h_rows, up_weight, preferred_element_type=jnp.float32)
    act_rows = (jax.nn.silu(gate) * up_proj).astype(jnp.bfloat16)
    return jnp.dot(act_rows, down_weight, preferred_element_type=jnp.float32)


def pair_rows(local, slot, half_side):
    shaped = local.reshape((2, half_side, local.shape[0] // (2 * half_side)) + local.shape[1:])
    picked = lax.dynamic_index_in_dim(shaped, slot, axis=1, keepdims=False)
    return picked.reshape((-1,) + local.shape[1:])


def keep_rows(x_in):
    return x_in


def skip_ffn(h_in):
    return jnp.zeros(h_in.shape, jnp.float32)


def solution(mesh):
    n_side = mesh.shape['side']
    half_side = n_side // 2
    to_ffn = [(slot, slot + half_side) for slot in range(half_side)]
    to_attn = [(slot + half_side, slot) for slot in range(half_side)]
    batch_axes = ('inst', 'dev')
    in_specs = (
        P(batch_axes, None),
        P(batch_axes),
        P(None, batch_axes, None, None, None),
        P(None, batch_axes, None, None, None),
        P(), P(), P(), P(), P(),
        P(None, None, 'dev'),
        P(None, None, 'dev'),
        P(None, 'dev', None),
    )
    out_specs = P(('inst', 'dev', 'side'), None)

    def device_fn(hidden, cache_len, k_cache, v_cache, w_q, w_kv, w_o, attn_gain, ffn_gain, w_gate, w_up, w_down):
        side_idx = lax.axis_index('side')
        is_attn = side_idx < half_side
        slot = side_idx % half_side
        rows = hidden.shape[0] // n_side
        n_layers = w_q.shape[0]
        x_pair = pair_rows(hidden, slot, half_side)
        lengths = pair_rows(cache_len, slot, half_side)
        for layer in range(n_layers):
            def attn_branch(x_in, layer=layer):
                k_seq = pair_rows(k_cache[layer], slot, half_side)
                v_seq = pair_rows(v_cache[layer], slot, half_side)
                return attention_layer(x_in, lengths, k_seq, v_seq, w_q[layer], w_kv[layer], w_o[layer], attn_gain[layer])

            def ffn_branch(h_in, layer=layer):
                return ffn_partial(h_in, w_gate[layer], w_up[layer], w_down[layer])

            x_pair = lax.cond(is_attn, attn_branch, keep_rows, x_pair)
            sent = lax.ppermute(x_pair, 'side', to_ffn)
            h_rows = rms_norm(sent, ffn_gain[layer])
            h_all = lax.all_gather(h_rows, 'dev', axis=0, tiled=True)
            part_sum = lax.cond(is_attn, skip_ffn, ffn_branch, h_all)
            summed = lax.psum_scatter(part_sum, 'dev', scatter_dimension=0, tiled=True)
            x_ffn = (sent.astype(jnp.float32) + summed.astype(jnp.bfloat16).astype(jnp.float32)).astype(jnp.bfloat16)
            if layer + 1 < n_layers:
                x_pair = lax.ppermute(x_ffn, 'side', to_attn)
            else:
                back = lax.ppermute(x_ffn[:rows], 'side', to_attn)
                out_rows = jnp.where(is_attn, back, x_ffn[rows:])
        return out_rows

    return jax.shard_map(device_fn, mesh=mesh, in_specs=in_specs, out_specs=out_specs, check_vma=False)
```

profile of v0, /device:TPU:0, one launch (start us, length us, event | category | flops | bytes accessed | tf_op | source)
XLA Modules:
  0.0 533.3 jit_solution(9878002226381188190)
XLA Ops:
  8.2 175.2 %conditional.2 = (bf16[128,4096]{1,0:T(8,128)(2,1)S(1)}) conditional(s32[]{:T(128)} %convert_element_type.68, bf16[128,4096]{1,0:T(8,128)(2,1)S(1)} %bitcast.111, (bf16[128,4096]{1,0:T(8,128)(2,1)S(1)}, s32[256]{0:T(256)}, f32[1,4096]{1,0:T(1,128)}, bf16[1,4096,4096]{2,1,0:T(8,128)(2,1)}, bf16[1,256,8,64,128]{4,3,2,1,0:T(8,128)(2,1)}, ...), branch_computations={%region_0.1_spmd, %region_1.5_spmd.clone} | conditional | flops 10889371648 | bytes 324974816 | solution.py:109
  8.5 20.8 %copy.49 = bf16[1,4096,2048]{1,2,0:T(8,128)(2,1)} copy(bf16[1,4096,2048]{2,1,0:T(8,128)(2,1)} %get-tuple-element.103) | data formatting | bytes 33554432 | tf_op jit(solution)/shard_map
  29.4 8.2 %fusion.27 = f32[128,2,8,128]{0,3,2,1:T(8,128)S(1)} fusion(bf16[2,8,128,4096]{3,2,1,0:T(8,128)(2,1)} %bitcast.109, bf16[128,4096]{1,0:T(8,128)(2,1)S(1)} %get-tuple-element.98, f32[4096]{0:T(1024)S(1)} %bitcast.120, f32[128]{0:T(128)S(1)} %add_rsqrt_fusion), kind=kOutput, calls=%fused_computation.25 | convolution fusion | flops 2149580800 | bytes 18891264 | tf_op jit(solution)/shard_map/cond/branch_1_fun/dot_general | solution.py:33
  39.3 44.3 %copy.48 = bf16[1,4096,4096]{1,2,0:T(8,128)(2,1)} copy(bf16[1,4096,4096]{2,1,0:T(8,128)(2,1)} %get-tuple-element.100) | data formatting | bytes 67108864 | tf_op jit(solution)/shard_map
  83.6 14.9 %fusion.29 = f32[128,32,128]{0,2,1:T(8,128)S(1)} fusion(bf16[32,128,4096]{2,1,0:T(8,128)(2,1)} %bitcast.108, bf16[128,4096]{1,0:T(8,128)(2,1)S(1)} %get-tuple-element.98, f32[4096]{0:T(1024)S(1)} %bitcast.121, f32[128]{0:T(128)S(1)} %add_rsqrt_fusion), kind=kOutput, calls=%fused_computation.27 | convolution fusion | flops 4297064448 | bytes 36717056 | tf_op jit(solution)/shard_map/cond/branch_1_fun/dot_general | solution.py:32
  99.8 1.8 copy.43
  101.7 2.6 copy.44
  104.3 2.6 pad_maximum_fusion
  106.9 3.4 fusion.42
  110.4 27.4 %constant_dynamic-slice_fusion.1 = (bf16[2,1,64,8,64,128]{5,4,3,2,1,0:T(8,128)(2,1)}, bf16[2,1,64,8,64,128]{5,4,3,2,1,0:T(8,128)(2,1)}) fusion(bf16[2,2,64,8,64,128]{5,4,3,2,1,0:T(8,128)(2,1)} %bitcast.115, s32[]{:T(128)S(6)} %select_n.34, bf16[2,2,64,8,64,128]{5,4,3,2,1,0:T(8,128)(2,1)} %bitcast.114), kind=kLoop, calls=%fused_computation.47 | loop fusion | bytes 67108864 | tf_op jit(solution)/shard_map/cond/branch_1_fun/jit(dynamic_index_in_dim)/dynamic_slice | solution.py:62
  137.9 12.8 %fusion.41 = (f32[128,8,4]{2,1,0:T(8,128)S(1)}, f32[128,8,4,64]{3,2,1,0:T(4,128)S(1)}) fusion(bf16[128,8,4,128]{3,2,1,0:T(4,128)(2,1)} %copy-done.5, bf16[128,8,64,128]{3,2,1,0:T(8,128)(2,1)} %bitcast.110, pred[128,64]{1,0:T(8,128)(4,1)S(1)} %iota_compare_fusion), kind=kOutput, calls=%fused_computation.61 | convolution fusion | flops 67891200 | bytes 18898944 | tf_op jit(solution)/shard_map/cond/branch_1_fun/nkgd,nksd->nkgs/dot_general | solution.py:38
  150.9 2.7 fusion.24
  154.7 1.9 fusion.35
  156.6 2.0 copy.47
  158.6 9.5 %fusion.23 = bf16[128,8,4,128]{3,2,1,0:T(4,128)(2,1)} fusion(bf16[128,8,64,128]{3,2,1,0:T(8,128)(2,1)} %bitcast.113, f32[128,8,4,64]{3,2,1,0:T(4,128)S(1)} %get-tuple-element.127, f32[128,8,4]{2,1,0:T(8,128)} %get-tuple-element.121, f32[128,8,128]{2,1,0:T(8,128)} %copy.47, f32[128,8,4]{2,1,0:T(8,128)} %get-tuple-element.120, f32[128,8,4]{2,1,0:T(8,128)} %copy-done.7), kind=kOutput, calls=%fused_computation.21 | convolution fusion | flops 69730304 | bytes 19447808 | tf_op jit(solution)/shard_map/cond/branch_1_fun/nkgs,nksd->nkgd/dot_general | solution.py:46
  168.1 1.8 reshape.162
  170.0 13.2 %fusion.17 = bf16[128,4096]{1,0:T(8,128)(2,1)S(1)} fusion(bf16[128,4096]{1,0:T(8,128)(2,1)S(1)} %reshape.162, bf16[1,4096,4096]{2,1,0:T(8,128)(2,1)} %get-tuple-element.105, bf16[128,4096]{1,0:T(8,128)(2,1)S(1)} %get-tuple-element.98), kind=kOutput, calls=%fused_computation.12 | convolution fusion | flops 4296540160 | bytes 36700160 | tf_op jit(solution)/shard_map/cond/branch_1_fun/dot_general | solution.py:49
  184.8 23.3 %collective-permute-done = bf16[128,4096]{1,0:T(8,128)(2,1)S(1)} collective-permute-done((bf16[128,4096]{1,0:T(8,128)(2,1)S(1)}, bf16[128,4096]{1,0:T(8,128)(2,1)S(1)}, u32[]{:S(2)}, u32[]{:S(2)}) %collective-permute-start) | collective-permute-done | bytes 1048608 | tf_op jit(solution)/shard_map/ppermute | solution.py:110
  209.7 83.3 %all-gather.2.cloned.1.call-done = bf16[512,4096]{1,0:T(8,128)(2,1)} async-done(((bf16[128,4096]{1,0:T(8,128)(2,1)}), bf16[512,4096]{1,0:T(8,128)(2,1)}) %all-gather.2.cloned.1.call-update) | async-done | bytes 4194320 | tf_op jit(solution)/shard_map/all_gather | solution.py:112
  293.1 6.2 %conditional.3 = (f32[512,4096]{1,0:T(8,128)}) conditional(s32[]{:T(128)} %convert_element_type.68, (bf16[1,4096,3584]{2,1,0:T(8,128)(2,1)}, bf16[512,4096]{1,0:T(8,128)(2,1)}, bf16[1,4096,3584]{2,1,0:T(8,128)(2,1)}, bf16[1,3584,4096]{2,1,0:T(8,128)(2,1)}) %tuple.18, () %tuple.19), branch_computations={%region_6.7_spmd, %region_7.8_spmd} | conditional | flops 45108166656 | bytes 126877704 | solution.py:113
  294.9 4.4 broadcast.103
  299.3 209.6 %reduce-scatter.2.cloned.1.call-done = f32[128,4096]{1,0:T(8,128)} async-done(((f32[512,4096]{1,0:T(8,128)}), f32[128,4096]{1,0:T(8,128)}) %reduce-scatter.2.cloned.1.call-update) | async-done | bytes 2097168 | tf_op jit(solution)/shard_map/reduce_scatter | solution.py:114
  508.9 1.8 fusion.40
  512.0 13.1 %collective-permute-done.1 = bf16[64,4096]{1,0:T(8,128)(2,1)S(1)} collective-permute-done((bf16[64,4096]{1,0:T(8,128)(2,1)S(1)}, bf16[64,4096]{1,0:T(8,128)(2,1)S(1)}, u32[]{:S(2)}, u32[]{:S(2)}) %collective-permute-start.1) | collective-permute-done | bytes 524320 | tf_op jit(solution)/shard_map/ppermute | solution.py:119
  (51 shorter events, 11.5 us)
Async XLA Ops:
  6.5 1.6 copy-start
  6.5 286.5 %all-gather.2.cloned.1.call-start = ((), (), s32[]{:S(2)}) async-start(), calls=%async_computation.1 | async-start | bytes 5242880 | tf_op jit(solution)/shard_map/all_gather | solution.py:112
  8.2 200.1 %copy-start.9 = (f32[1,4096]{1,0:T(1,128)S(1)}, f32[1,4096]{1,0:T(1,128)}, u32[]{:S(2)}) copy-start(f32[1,4096]{1,0:T(1,128)} %param.24) | copy-start | bytes 49156
  8.5 20.8 %copy-start.8 = (f32[1,4096]{1,0:T(1,128)S(1)}, f32[1,4096]{1,0:T(1,128)}, u32[]{:S(2)}) copy-start(f32[1,4096]{1,0:T(1,128)} %get-tuple-element.99) | copy-start | bytes 49156 | tf_op jit(solution)/shard_map/cond
  29.4 8.3 %copy-start.10 = (s32[256]{0:T(256)S(1)}, s32[256]{0:T(256)}, u32[]{:S(2)}) copy-start(s32[256]{0:T(256)} %get-tuple-element.107) | copy-start | bytes 3076 | tf_op jit(solution)/shard_map/cond
  37.6 46.0 %copy-start.4 = (f32[128,2,8,128]{0,3,2,1:T(8,128)}, f32[128,2,8,128]{0,3,2,1:T(8,128)S(1)}, u32[]{:S(2)}) copy-start(f32[128,2,8,128]{0,3,2,1:T(8,128)S(1)} %fusion.27) | copy-start | bytes 3145732 | tf_op jit(solution)/shard_map/cond
  106.9 30.9 %copy-start.5 = (bf16[128,8,4,128]{3,2,1,0:T(4,128)(2,1)}, bf16[128,8,4,128]{3,2,1,0:T(4,128)(2,1)S(1)}, u32[]{:S(2)}) copy-start(bf16[128,8,4,128]{3,2,1,0:T(4,128)(2,1)S(1)} %pad_maximum_fusion) | copy-start | bytes 3145732 | tf_op jit(solution)/shard_map/cond
  137.9 12.8 %copy-start.6 = (f32[128,8,1,4]{3,2,1,0:T(1,128)S(1)}, f32[128,8,1,4]{3,2,1,0:T(1,128)}, u32[]{:S(2)}) copy-start(f32[128,8,1,4]{3,2,1,0:T(1,128)} %fusion.42) | copy-start | bytes 49156 | tf_op jit(solution)/shard_map/cond
  150.9 3.8 copy-start.7
  183.4 24.6 %collective-permute-start = (bf16[128,4096]{1,0:T(8,128)(2,1)S(1)}, bf16[128,4096]{1,0:T(8,128)(2,1)S(1)}, u32[]{:S(2)}, u32[]{:S(2)}) collective-permute-start(bf16[128,4096]{1,0:T(8,128)(2,1)S(1)} %get-tuple-element.130), channel_id=1, source_target_pairs={{0,2},{1,3},{4,6},{5,7},{8,10},{9,11},{12,14},{13,15},{16,18},{17,... | collective-permute-start | bytes 3145736 | tf_op jit(solution)/shard_map/ppermute | solution.py:110
  208.0 85.0 %copy-start.2 = (bf16[128,4096]{1,0:T(8,128)(2,1)}, bf16[128,4096]{1,0:T(8,128)(2,1)S(1)}, u32[]{:S(2)}) copy-start(bf16[128,4096]{1,0:T(8,128)(2,1)S(1)} %collective-permute-done) | copy-start | bytes 3145732
  209.7 299.2 %reduce-scatter.2.cloned.1.call-start = ((), (), s32[]{:S(2)}) async-start(), calls=%async_computation.2 | async-start | bytes 10485760 | tf_op jit(solution)/shard_map/reduce_scatter | solution.py:114
  299.2 209.6 %copy-start.3 = (bf16[128,4096]{1,0:T(8,128)(2,1)S(1)}, bf16[128,4096]{1,0:T(8,128)(2,1)}, u32[]{:S(2)}) copy-start(bf16[128,4096]{1,0:T(8,128)(2,1)} %copy-done.2) | copy-start | bytes 3145732
  299.3 226.7 %copy-start.1 = (bf16[256,4096]{1,0:T(8,128)(2,1)S(1)}, bf16[256,4096]{1,0:T(8,128)(2,1)}, u32[]{:S(2)}) copy-start(bf16[256,4096]{1,0:T(8,128)(2,1)} %param.16) | copy-start | bytes 6291460
  510.7 14.4 %collective-permute-start.1 = (bf16[64,4096]{1,0:T(8,128)(2,1)S(1)}, bf16[64,4096]{1,0:T(8,128)(2,1)S(1)}, u32[]{:S(2)}, u32[]{:S(2)}) collective-permute-start(bf16[64,4096]{1,0:T(8,128)(2,1)S(1)} %slice.39), channel_id=1, source_target_pairs={{2,0},{3,1},{6,4},{7,5},{10,8},{11,9},{14,12},{15,13},{18,16},{19,... | collective-permute-start | bytes 1572872 | tf_op jit(solution)/shard_map/ppermute | solution.py:119
Sparse Core Ops, SparseCore 0:
  209.8 83.2 all-gather.1
  299.4 209.4 reduce-scatter.1
where the time goes:
time: 543 us; the launch traced here: 533 us
  waiting for transfers between devices  329 us (61%)
  local copies, waits for them, and re-layouts  108 us (20%)
  matrix products  62.1 us (11%)
  other arithmetic  14.7 us (3%)
  between operations  14 us (3%)
    reduce_scatter x1, waiting for transfers between devices, device_fn(): summed = lax.psum_scatter(part_sum, 'dev', scatter_dimension=0, tiled=True)  210 us
    all_gather x1, waiting for transfers between devices, device_fn(): h_all = lax.all_gather(h_rows, 'dev', axis=0, tiled=True)  83.3 us
    another operation x3, local copies, waits for them, and re-layouts  69.5 us
    dynamic_slice x3, local copies, waits for them, and re-layouts, pair_rows(): picked = lax.dynamic_index_in_dim(shaped, slot, axis=1, keepdims=False)  27.5 us
    ppermute x1, waiting for transfers between devices, device_fn(): sent = lax.ppermute(x_pair, 'side', to_ffn)  23.3 us
    dot_general x1, matrix products, attention_layer(): jnp.dot(normed, q_weight, preferred_element_type=jnp.float32)  14.9 us
    dot_general x1, matrix products, attention_layer(): attn_out = jnp.dot(mixed, o_weight, preferred_element_type=jnp.float32)  13.2 us
    ppermute x1, waiting for transfers between devices, device_fn(): back = lax.ppermute(x_ffn[:rows], 'side', to_attn)  13.1 us
  transfers between devices with their start and end apart: 4, of which 4 were waited for; matrix products, arithmetic and copies ran while one was open for 0% of the time, Pallas kernels for 0%

commit v1 on v0

--- a/solution.py
+++ b/solution.py
@@ -57,25 +57,13 @@
     return jnp.dot(act_rows, down_weight, preferred_element_type=jnp.float32)
 
 
-def pair_rows(local, slot, half_side):
-    shaped = local.reshape((2, half_side, local.shape[0] // (2 * half_side)) + local.shape[1:])
-    picked = lax.dynamic_index_in_dim(shaped, slot, axis=1, keepdims=False)
-    return picked.reshape((-1,) + local.shape[1:])
-
-
-def keep_rows(x_in):
-    return x_in
-
-
-def skip_ffn(h_in):
-    return jnp.zeros(h_in.shape, jnp.float32)
+def own_rows(local, side_idx, n_side):
+    rows = local.shape[0] // n_side
+    return lax.dynamic_slice_in_dim(local, side_idx * rows, rows, axis=0)
 
 
 def solution(mesh):
     n_side = mesh.shape['side']
-    half_side = n_side // 2
-    to_ffn = [(slot, slot + half_side) for slot in range(half_side)]
-    to_attn = [(slot + half_side, slot) for slot in range(half_side)]
     batch_axes = ('inst', 'dev')
     in_specs = (
         P(batch_axes, None),
@@ -91,33 +79,17 @@
 
     def device_fn(hidden, cache_len, k_cache, v_cache, w_q, w_kv, w_o, attn_gain, ffn_gain, w_gate, w_up, w_down):
         side_idx = lax.axis_index('side')
-        is_attn = side_idx < half_side
-        slot = side_idx % half_side
-        rows = hidden.shape[0] // n_side
-        n_layers = w_q.shape[0]
-        x_pair = pair_rows(hidden, slot, half_side)
-        lengths = pair_rows(cache_len, slot, half_side)
-        for layer in range(n_layers):
-            def attn_branch(x_in, layer=layer):
-                k_seq = pair_rows(k_cache[layer], slot, half_side)
-                v_seq = pair_rows(v_cache[layer], slot, half_side)
-                return attention_layer(x_in, lengths, k_seq, v_seq, w_q[layer], w_kv[layer], w_o[layer], attn_gain[layer])
-
-            def ffn_branch(h_in, layer=layer):
-                return ffn_partial(h_in, w_gate[layer], w_up[layer], w_down[layer])
-
-            x_pair = lax.cond(is_attn, attn_branch, keep_rows, x_pair)
-            sent = lax.ppermute(x_pair, 'side', to_ffn)
-            h_rows = rms_norm(sent, ffn_gain[layer])
+        x_rows = own_rows(hidden, side_idx, n_side)
+        lengths = own_rows(cache_len, side_idx, n_side)
+        for layer in range(w_q.shape[0]):
+            k_seq = own_rows(k_cache[layer], side_idx, n_side)
+            v_seq = own_rows(v_cache[layer], side_idx, n_side)
+            x_mid = attention_layer(x_rows, lengths, k_seq, v_seq, w_q[layer], w_kv[layer], w_o[layer], attn_gain[layer])
+            h_rows = rms_norm(x_mid, ffn_gain[layer])
             h_all = lax.all_gather(h_rows, 'dev', axis=0, tiled=True)
-            part_sum = lax.cond(is_attn, skip_ffn, ffn_branch, h_all)
+            part_sum = ffn_partial(h_all, w_gate[layer], w_up[layer], w_down[layer])
             summed = lax.psum_scatter(part_sum, 'dev', scatter_dimension=0, tiled=True)
-            x_ffn = (sent.astype(jnp.float32) + summed.astype(jnp.bfloat16).astype(jnp.float32)).astype(jnp.bfloat16)
-            if layer + 1 < n_layers:
-                x_pair = lax.ppermute(x_ffn, 'side', to_attn)
-            else:
-                back = lax.ppermute(x_ffn[:rows], 'side', to_attn)
-                out_rows = jnp.where(is_attn, back, x_ffn[rows:])
-        return out_rows
+            x_rows = (x_mid.astype(jnp.float32) + summed.astype(jnp.bfloat16).astype(jnp.float32)).astype(jnp.bfloat16)
+        return x_rows
 
     return jax.shard_map(device_fn, mesh=mesh, in_specs=in_specs, out_specs=out_specs, check_vma=False)

time: 543 us -> 311 us (0.57); the launches traced: 533 us -> 309 us
  waiting for transfers between devices: 329 us -> 124 us
  local copies, waits for them, and re-layouts: 108 us -> 63.3 us
  matrix products: 62.1 us -> 101 us
  other arithmetic: 14.7 us -> 6.88 us
    reduce_scatter x1, waiting for transfers between devices: 210 us -> 75.9 us  [device_fn(): summed = lax.psum_scatter(part_sum, 'dev', scatter_dimension=0, tiled=True)]
    another operation x3 -> x0, local copies, waits for them, and re-layouts: 69.5 us -> none
    dot_general x0 -> x2, local copies, waits for them, and re-layouts: none -> 61.9 us  [the longest x1 41 us: attention_layer(): jnp.dot(normed, q_weight, preferred_element_type=jnp.float32)]
    dot_general x0 -> x2, matrix products: none -> 49.1 us  [the longest x1 30.1 us: ffn_partial(): return jnp.dot(act_rows, down_weight, preferred_element_type=jnp.float32)]
    ppermute x2 -> x0, waiting for transfers between devices: 36.3 us -> none  [the longest x1 23.3 us: device_fn(): sent = lax.ppermute(x_pair, 'side', to_ffn)]
    all_gather x1, waiting for transfers between devices: 83.3 us -> 48.1 us  [device_fn(): h_all = lax.all_gather(h_rows, 'dev', axis=0, tiled=True)]
    dynamic_slice x3 -> x0, local copies, waits for them, and re-layouts: 27.5 us -> none  [pair_rows(): picked = lax.dynamic_index_in_dim(shaped, slot, axis=1, keepdims=False)]
  transfers between devices with their start and end apart: 4 -> 2, of which waited for: 4 -> 2; matrix products, arithmetic and copies ran while one was open for 0% -> 0% of each run, Pallas kernels for 0% -> 0%
where the time goes in v1:
time: 311 us; the launch traced here: 309 us
  waiting for transfers between devices  124 us (40%)
  matrix products  101 us (32%)
  local copies, waits for them, and re-layouts  63.3 us (20%)
  between operations  13.6 us (4%)
  other arithmetic  6.88 us (2%)
    reduce_scatter x1, waiting for transfers between devices, device_fn(): summed = lax.psum_scatter(part_sum, 'dev', scatter_dimension=0, tiled=True)  75.9 us
    all_gather x1, waiting for transfers between devices, device_fn(): h_all = lax.all_gather(h_rows, 'dev', axis=0, tiled=True)  48.1 us
    dot_general x1, local copies, waits for them, and re-layouts, attention_layer(): jnp.dot(normed, q_weight, preferred_element_type=jnp.float32)  41 us
    dot_general x1, matrix products, ffn_partial(): return jnp.dot(act_rows, down_weight, preferred_element_type=jnp.float32)  30.1 us
    dot_general x1, local copies, waits for them, and re-layouts, attention_layer(): jnp.dot(normed, kv_weight, preferred_element_type=jnp.float32)  20.8 us
    dot_general x1, matrix products, ffn_partial(): gate = jnp.dot(h_rows, gate_weight, preferred_element_type=jnp.float32)  19 us
    dot_general x1, matrix products, attention_layer(): jnp.dot(normed, q_weight, preferred_element_type=jnp.float32)  15.6 us
    dot_general x1, matrix products, attention_layer(): attn_out = jnp.dot(mixed, o_weight, preferred_element_type=jnp.float32)  14 us
  transfers between devices with their start and end apart: 2, of which 2 were waited for; matrix products, arithmetic and copies ran while one was open for 0% of the time, Pallas kernels for 0%

profile of v1, /device:TPU:0, one launch (start us, length us, event | category | flops | bytes accessed | tf_op | source)
XLA Modules:
  0.0 309.3 jit_solution(18217005764121317067)
XLA Ops:
  6.6 1.2 fusion.38
  7.8 20.8 %copy.22 = bf16[2048,4096]{1,0:T(8,128)(2,1)} copy(bf16[2048,4096]{0,1:T(8,128)(2,1)} %bitcast.88) | data formatting | bytes 33554432 | tf_op jit(solution)/shard_map/dot_general | solution.py:33
  28.7 8.8 %fusion.46 = f32[64,2,8,128]{3,0,2,1:T(8,128)S(1)} fusion(bf16[2,8,128,4096]{3,2,1,0:T(8,128)(2,1)} %bitcast.86, f32[4096]{0:T(1024)S(1)} %bitcast.93, f32[64]{0:T(128)S(1)} %add_rsqrt_fusion.1, bf16[256,4096]{1,0:T(8,128)(2,1)S(1)} %copy-done, s32[]{:T(128)S(6)} %select_n.10), kind=kOutput, calls=%fused_computation.37 | convolution fusion | flops 1074790400 | bytes 17842692 | tf_op jit(solution)/shard_map/dot_general | solution.py:33
  37.5 41.0 %copy.21 = bf16[4096,4096]{1,0:T(8,128)(2,1)} copy(bf16[4096,4096]{0,1:T(8,128)(2,1)} %bitcast.87) | data formatting | bytes 67108864 | tf_op jit(solution)/shard_map/dot_general | solution.py:32
  78.5 15.6 %fusion.48 = f32[64,32,128]{2,0,1:T(8,128)S(1)} fusion(bf16[32,128,4096]{2,1,0:T(8,128)(2,1)} %bitcast.85, f32[4096]{0:T(1024)S(1)} %bitcast.94, f32[64]{0:T(128)S(1)} %add_rsqrt_fusion.1, bf16[256,4096]{1,0:T(8,128)(2,1)S(1)} %copy-done, s32[]{:T(128)S(6)} %select_n.10), kind=kOutput, calls=%fused_computation.39 | convolution fusion | flops 2148532224 | bytes 35144196 | tf_op jit(solution)/shard_map/dot_general | solution.py:32
  94.2 0.2 multiply_cosine_fusion
  94.4 0.4 subtract_convert_fusion
  94.9 0.4 copy.15
  95.3 0.4 copy.14
  95.8 0.2 subtract_convert_fusion.1
  96.0 0.1 maximum_bitcast_fusion
  96.1 0.9 fusion.51
  97.0 8.1 %fusion.63 = (f32[64,8,4]{2,1,0:T(8,128)S(1)}, f32[64,8,4,64]{3,2,1,0:T(4,128)S(1)}) fusion(bf16[1,256,8,64,128]{4,3,2,1,0:T(8,128)(2,1)} %param.14, s32[]{:T(128)S(6)} %select_n.10, bf16[64,8,4,64]{3,2,1,0:T(4,128)(2,1)S(1)} %copy.15, bf16[64,8,4,64]{3,2,1,0:T(4,128)(2,1)S(1)} %copy.14, pred[64,64]{1,0:T(8,128)(4,1)S(1)} %iota_compare_fusion), kind=kOutput, calls=%fused_computation.66 | convolution fusion | flops 34994176 | bytes 9449476 | tf_op jit(solution)/shard_map/nkgd,nksd->nkgs/dot_general | solution.py:38
  105.1 1.3 fusion.41
  106.5 0.2 copy.17
  106.7 5.1 %divide_convert_fusion = bf16[64,8,4,128]{3,2,1,0:T(4,128)(2,1)S(1)} fusion(bf16[1,256,8,64,128]{4,3,2,1,0:T(8,128)(2,1)} %param.15, s32[]{:T(128)S(6)} %select_n.10, f32[64,8,4,64]{3,2,1,0:T(4,128)S(1)} %get-tuple-element.16, f32[64,8,4]{2,1,0:T(8,128)S(1)} %get-tuple-element.10, f32[64,8,128]{2,1,0:T(8,128)S(1)} %copy.17, ...), kind=kOutput, calls=%fused_computation.33 | convolution fusion | flops 34865152 | bytes 9723908 | tf_op jit(solution)/shard_map/nkgs,nksd->nkgd/dot_general | solution.py:46
  111.7 0.4 reshape.123
  112.1 14.0 %multiply_reduce_fusion = (f32[64]{0:T(128)S(1)}, f32[64,4096]{1,0:T(8,128)S(1)}) fusion(bf16[64,4096]{1,0:T(8,128)(2,1)S(1)} %reshape.123, bf16[1,4096,4096]{2,1,0:T(8,128)(2,1)} %param.18, bf16[256,4096]{1,0:T(8,128)(2,1)} %param.12, s32[]{:T(128)S(6)} %select_n.10), kind=kOutput, calls=%fused_computation.29 | convolution fusion | flops 2149056512 | bytes 35651844 | tf_op jit(solution)/shard_map/dot_general | solution.py:49
  126.1 1.0 multiply_convert_fusion
  127.2 48.1 %all-gather.2.cloned.1.call-done = bf16[256,4096]{1,0:T(8,128)(2,1)} async-done(((bf16[64,4096]{1,0:T(8,128)(2,1)}), bf16[256,4096]{1,0:T(8,128)(2,1)}) %all-gather.2.cloned.1.call-update) | async-done | bytes 2097168 | tf_op jit(solution)/shard_map/all_gather | solution.py:89
  175.3 19.0 %fusion.6 = f32[256,3584]{1,0:T(8,128)} fusion(bf16[256,4096]{1,0:T(8,128)(2,1)} %all-gather.2.cloned.1.call-done, bf16[1,4096,3584]{2,1,0:T(8,128)(2,1)} %param.21), kind=kOutput, calls=%fused_computation.6 | convolution fusion | flops 7516192768 | bytes 35127296 | tf_op jit(solution)/shard_map/dot_general | solution.py:54
  194.3 30.1 %fusion.2 = f32[256,4096]{1,0:T(8,128)} fusion(bf16[1,3584,4096]{2,1,0:T(8,128)(2,1)} %param.23, bf16[256,4096]{1,0:T(8,128)(2,1)S(1)} %copy-done.4, bf16[1,4096,3584]{2,1,0:T(8,128)(2,1)} %param.22, f32[256,3584]{1,0:T(8,128)} %fusion.6), kind=kOutput, calls=%fused_computation.2 | convolution fusion | flops 15037890560 | bytes 68681728 | tf_op jit(solution)/shard_map/dot_general | solution.py:57
  224.4 75.9 %reduce-scatter.2.cloned.1.call-done = f32[64,4096]{1,0:T(8,128)} async-done(((f32[256,4096]{1,0:T(8,128)}), f32[64,4096]{1,0:T(8,128)}) %reduce-scatter.2.cloned.1.call-update) | async-done | bytes 1048592 | tf_op jit(solution)/shard_map/reduce_scatter | solution.py:91
  300.3 2.1 add_convert_fusion
  (23 shorter events, 0.4 us)
Async XLA Ops:
  6.5 168.8 %all-gather.2.cloned.1.call-start = ((), (), s32[]{:S(2)}) async-start(), calls=%async_computation.1 | async-start | bytes 2621440 | tf_op jit(solution)/shard_map/all_gather | solution.py:89
  7.8 20.9 %copy-start = (bf16[256,4096]{1,0:T(8,128)(2,1)S(1)}, bf16[256,4096]{1,0:T(8,128)(2,1)}, u32[]{:S(2)}) copy-start(bf16[256,4096]{1,0:T(8,128)(2,1)} %param.12) | copy-start | bytes 6291460
  7.8 20.9 %copy-start.1 = (f32[1,4096]{1,0:T(1,128)S(1)}, f32[1,4096]{1,0:T(1,128)}, u32[]{:S(2)}) copy-start(f32[1,4096]{1,0:T(1,128)} %param.19) | copy-start | bytes 49156
  78.5 15.6 %copy-start.3 = (s32[256]{0:T(256)S(1)}, s32[256]{0:T(256)}, u32[]{:S(2)}) copy-start(s32[256]{0:T(256)} %param.13) | copy-start | bytes 3076
  112.1 14.0 %copy-start.2 = (f32[1,4096]{1,0:T(1,128)S(1)}, f32[1,4096]{1,0:T(1,128)}, u32[]{:S(2)}) copy-start(f32[1,4096]{1,0:T(1,128)} %param.20) | copy-start | bytes 49156
  127.1 173.2 %reduce-scatter.2.cloned.1.call-start = ((), (), s32[]{:S(2)}) async-start(), calls=%async_computation.2 | async-start | bytes 5242880 | tf_op jit(solution)/shard_map/reduce_scatter | solution.py:91
  175.3 19.0 %copy-start.4 = (bf16[256,4096]{1,0:T(8,128)(2,1)S(1)}, bf16[256,4096]{1,0:T(8,128)(2,1)}, u32[]{:S(2)}) copy-start(bf16[256,4096]{1,0:T(8,128)(2,1)} %all-gather.2.cloned.1.call-done) | copy-start | bytes 6291460
Sparse Core Ops, SparseCore 0:
  127.3 48.0 all-gather.1
  224.6 75.6 reduce-scatter.1

commit v2 on v1

v2 whole, which is shorter than its diff:
```python
import functools

import jax
import jax.numpy as jnp
from jax import lax
from jax.experimental import pallas as pl
from jax.experimental.pallas import tpu as pltpu
from jax.sharding import PartitionSpec as P

EPS = 1e-5
ROPE_BASE = 10000.0
TILE = 512
SLOTS = 10
SEQS = 8
KV_BUFS = 3
VMEM_LIMIT = 66_000_000


def attention_kernel(rows, x_ref, gain_ref, ffn_gain_ref, cos_ref, sin_ref, len_ref, k_hbm, v_hbm, wq_hbm, wkv_hbm,
                     wo_hbm, x1_ref, h_ref, ring, k_buf, v_buf, a_s, q_s, kv_s, o_s, ob_s, tq, tk, tv, to,
                     w_sem, k_sem, v_sem):
    width = x_ref.shape[1]
    kv_heads, cache, head = k_hbm.shape[1:]
    n_q = wq_hbm.shape[1] // TILE
    n_kv = wkv_hbm.shape[1] // TILE
    n_o = wo_hbm.shape[1] // TILE
    heads = wq_hbm.shape[1] // head
    group = heads // kv_heads
    n_groups = rows // SEQS
    base = lax.axis_index('side') * rows

    def weight_copy(hbm, tile, slot):
        cols = pl.ds(pl.multiple_of(tile * TILE, TILE), TILE)
        return pltpu.make_async_copy(hbm.at[:, cols], ring.at[slot], w_sem.at[slot])

    def kv_copies(g):
        buf = lax.rem(g, KV_BUFS)
        seqs = pl.ds(base + g * SEQS, SEQS)
        return (pltpu.make_async_copy(k_hbm.at[seqs], k_buf.at[buf], k_sem.at[buf]),
                pltpu.make_async_copy(v_hbm.at[seqs], v_buf.at[buf], v_sem.at[buf]))

    def start_kv(g):
        for copy in kv_copies(g):
            copy.start()

    def start_seq(i):
        slot = lax.rem(i, SLOTS)

        @pl.when(i < n_q)
        def _():
            weight_copy(wq_hbm, i, slot).start()

        @pl.when((i >= n_q) & (i < n_q + n_kv))
        def _():
            weight_copy(wkv_hbm, i - n_q, slot).start()

        @pl.when((i >= n_q + n_kv) & (i < n_q + n_kv + n_o))
        def _():
            weight_copy(wo_hbm, i - n_q - n_kv, slot).start()

    def first(i, carry):
        start_seq(i)
        return carry

    lax.fori_loop(0, SLOTS, first, 0)
    for g in range(KV_BUFS):
        start_kv(g)

    x_f = x_ref[...].astype(jnp.float32)
    inv = lax.rsqrt(jnp.mean(x_f * x_f, axis=-1, keepdims=True) + EPS)
    a_s[...] = (x_f * inv * gain_ref[...]).astype(jnp.bfloat16)

    def rotated(tile, i):
        vec = tile[:, i * head:(i + 1) * head]
        return vec * cos_ref[...] + pltpu.roll(vec, head // 2, 1) * sin_ref[...]

    def q_step(t, carry):
        slot = lax.rem(t, SLOTS)
        weight_copy(wq_hbm, t, slot).wait()
        tile = jnp.dot(a_s[...], ring[slot], preferred_element_type=jnp.float32)
        for i in range(TILE // head):
            q_s[:, pl.ds(pl.multiple_of(t * TILE + i * head, head), head)] = rotated(tile, i)
        start_seq(t + SLOTS)
        return carry

    lax.fori_loop(0, n_q, q_step, 0)

    def kv_step(t, carry):
        slot = lax.rem(t + n_q, SLOTS)
        weight_copy(wkv_hbm, t, slot).wait()
        tile = jnp.dot(a_s[...], ring[slot], preferred_element_type=jnp.float32)

        @pl.when(t < n_kv // 2)
        def _():
            for i in range(TILE // head):
                kv_s[:, pl.ds(pl.multiple_of(t * TILE + i * head, head), head)] = rotated(tile, i)

        @pl.when(t >= n_kv // 2)
        def _():
            kv_s[:, pl.ds(pl.multiple_of(t * TILE, TILE), TILE)] = tile

        start_seq(t + n_q + SLOTS)
        return carry

    lax.fori_loop(0, n_kv, kv_step, 0)

    scale = head ** -0.5
    keys = kv_heads * cache
    row_head = lax.broadcasted_iota(jnp.int32, (heads, keys), 0) // group
    col = lax.broadcasted_iota(jnp.int32, (heads, keys), 1)
    key_pos = jnp.where(col // cache == row_head, col % cache, cache + 1)
    own = (lax.broadcasted_iota(jnp.int32, (heads, kv_heads), 0) // group
           == lax.broadcasted_iota(jnp.int32, (heads, kv_heads), 1))
    nt = (((1,), (1,)), ((), ()))

    def kv_group(g, carry):
        buf = lax.rem(g, KV_BUFS)
        block = pl.ds(pl.multiple_of(g * SEQS, SEQS), SEQS)
        for h in range(heads):
            tq[pl.ds(h, SEQS, stride=heads), :] = q_s[block, h * head:(h + 1) * head]
        for h in range(kv_heads):
            tk[pl.ds(h, SEQS, stride=kv_heads), :] = kv_s[block, h * head:(h + 1) * head]
            off = (kv_heads + h) * head
            tv[pl.ds(h, SEQS, stride=kv_heads), :] = kv_s[block, off:off + head]
        for copy in kv_copies(g):
            copy.wait()
        for i in range(SEQS):
            n = len_ref[g * SEQS + i]
            q = tq[i * heads:(i + 1) * heads, :].astype(jnp.bfloat16)
            k_new = tk[i * kv_heads:(i + 1) * kv_heads, :].astype(jnp.bfloat16)
            v_new = tv[i * kv_heads:(i + 1) * kv_heads, :].astype(jnp.bfloat16)
            k = k_buf[buf, i].reshape(keys, head)
            v = v_buf[buf, i].reshape(keys, head)
            s = lax.dot_general(q, k, nt, preferred_element_type=jnp.float32) * scale
            s = jnp.where(key_pos < n, s, -1e30)
            s_own = lax.dot_general(q, k_new, nt, preferred_element_type=jnp.float32) * scale
            s_own = jnp.max(jnp.where(own, s_own, -jnp.inf), axis=-1, keepdims=True)
            top = jnp.maximum(jnp.max(s, axis=-1, keepdims=True), s_own)
            e = jnp.exp(s - top)
            e_own = jnp.exp(s_own - top)
            total = jnp.sum(e, axis=-1, keepdims=True) + e_own
            mixed = jnp.dot(e.astype(jnp.bfloat16), v, preferred_element_type=jnp.float32)
            spread = jnp.where(own, e_own, 0.0).astype(jnp.bfloat16)
            mixed += jnp.dot(spread, v_new, preferred_element_type=jnp.float32)
            to[i * heads:(i + 1) * heads, :] = mixed / total
        for h in range(heads):
            o_s[block, h * head:(h + 1) * head] = to[pl.ds(h, SEQS, stride=heads), :]

        @pl.when(g + KV_BUFS < n_groups)
        def _():
            start_kv(g + KV_BUFS)

        return carry

    lax.fori_loop(0, n_groups, kv_group, 0)
    ob_s[...] = o_s[...].astype(jnp.bfloat16)

    def o_step(t, square):
        slot = lax.rem(t + n_q + n_kv, SLOTS)
        weight_copy(wo_hbm, t, slot).wait()
        tile = jnp.dot(ob_s[...], ring[slot], preferred_element_type=jnp.float32)
        cols = pl.ds(pl.multiple_of(t * TILE, TILE), TILE)
        x1 = (x_ref[:, cols].astype(jnp.float32) + tile).astype(jnp.bfloat16)
        x1_ref[:, cols] = x1
        x1_f = x1.astype(jnp.float32)
        return square + jnp.sum(x1_f * x1_f, axis=-1, keepdims=True)

    square = lax.fori_loop(0, n_o, o_step, jnp.zeros((rows, 1), jnp.float32))
    inv = lax.rsqrt(square / width + EPS)
    h_ref[...] = (x1_ref[...].astype(jnp.float32) * inv * ffn_gain_ref[...]).astype(jnp.bfloat16)


def attention(x_rows, lengths, k_cache, v_cache, w_q, w_kv, w_o, gain_attn, gain_ffn):
    rows, width = x_rows.shape
    _, kv_heads, cache, head = k_cache.shape
    heads = w_q.shape[1] // head
    half = head // 2
    freqs = ROPE_BASE ** (-jnp.arange(half, dtype=jnp.float32) / half)
    angle = lengths.astype(jnp.float32)[:, None] * freqs
    cos_part, sin_part = jnp.cos(angle), jnp.sin(angle)
    cos_full = jnp.concatenate([cos_part, cos_part], axis=-1)
    sin_full = jnp.concatenate([-sin_part, sin_part], axis=-1)
    vmem = pl.BlockSpec(memory_space=pltpu.VMEM)
    hbm = pl.BlockSpec(memory_space=pl.ANY)
    row_block = jax.ShapeDtypeStruct((rows, width), jnp.bfloat16)
    weights = w_q.size + w_kv.size + w_o.size
    return pl.pallas_call(
        functools.partial(attention_kernel, rows),
        out_shape=(row_block, row_block),
        in_specs=[vmem] * 5 + [pl.BlockSpec(memory_space=pltpu.SMEM)] + [hbm] * 5,
        out_specs=(vmem, vmem),
        scratch_shapes=[
            pltpu.VMEM((SLOTS, width, TILE), jnp.bfloat16),
            pltpu.VMEM((KV_BUFS, SEQS, kv_heads, cache, head), jnp.bfloat16),
            pltpu.VMEM((KV_BUFS, SEQS, kv_heads, cache, head), jnp.bfloat16),
            pltpu.VMEM((rows, width), jnp.bfloat16),
            pltpu.VMEM((rows, heads * head), jnp.float32),
            pltpu.VMEM((rows, 2 * kv_heads * head), jnp.float32),
            pltpu.VMEM((rows, heads * head), jnp.float32),
            pltpu.VMEM((rows, heads * head), jnp.bfloat16),
            pltpu.VMEM((SEQS * heads, head), jnp.float32),
            pltpu.VMEM((SEQS * kv_heads, head), jnp.float32),
            pltpu.VMEM((SEQS * kv_heads, head), jnp.float32),
            pltpu.VMEM((SEQS * heads, head), jnp.float32),
            pltpu.SemaphoreType.DMA((SLOTS,)),
            pltpu.SemaphoreType.DMA((KV_BUFS,)),
            pltpu.SemaphoreType.DMA((KV_BUFS,)),
        ],
        compiler_params=pltpu.CompilerParams(vmem_limit_bytes=VMEM_LIMIT),
        cost_estimate=pl.CostEstimate(flops=2 * rows * weights, bytes_accessed=2 * weights, transcendentals=0),
        name="attention",
    )(x_rows, gain_attn[None], gain_ffn[None], cos_full, sin_full, lengths, k_cache, v_cache, w_q, w_kv, w_o)


def ffn_partial(h_rows, gate_weight, up_weight, down_weight):
    gate = jnp.dot(h_rows, gate_weight, preferred_element_type=jnp.float32)
    up_proj = jnp.dot(h_rows, up_weight, preferred_element_type=jnp.float32)
    act_rows = (jax.nn.silu(gate) * up_proj).astype(jnp.bfloat16)
    return jnp.dot(act_rows, down_weight, preferred_element_type=jnp.float32)


def own_rows(local, side_idx, n_side):
    rows = local.shape[0] // n_side
    return lax.dynamic_slice_in_dim(local, side_idx * rows, rows, axis=0)


def solution(mesh):
    n_side = mesh.shape['side']
    batch_axes = ('inst', 'dev')
    in_specs = (
        P(batch_axes, None),
        P(batch_axes),
        P(None, batch_axes, None, None, None),
        P(None, batch_axes, None, None, None),
        P(), P(), P(), P(), P(),
        P(None, None, 'dev'),
        P(None, None, 'dev'),
        P(None, 'dev', None),
    )
    out_specs = P(('inst', 'dev', 'side'), None)

    def device_fn(hidden, cache_len, k_cache, v_cache, w_q, w_kv, w_o, attn_gain, ffn_gain, w_gate, w_up, w_down):
        side_idx = lax.axis_index('side')
        x_rows = own_rows(hidden, side_idx, n_side)
        lengths = own_rows(cache_len, side_idx, n_side)
        for layer in range(w_q.shape[0]):
            x_mid, h_rows = attention(x_rows, lengths, k_cache[layer], v_cache[layer], w_q[layer], w_kv[layer], w_o[layer],
                                      attn_gain[layer], ffn_gain[layer])
            h_all = lax.all_gather(h_rows, 'dev', axis=0, tiled=True)
            part_sum = ffn_partial(h_all, w_gate[layer], w_up[layer], w_down[layer])
            summed = lax.psum_scatter(part_sum, 'dev', scatter_dimension=0, tiled=True)
            x_rows = (x_mid.astype(jnp.float32) + summed.astype(jnp.bfloat16).astype(jnp.float32)).astype(jnp.bfloat16)
        return x_rows

    return jax.shard_map(device_fn, mesh=mesh, in_specs=in_specs, out_specs=out_specs, check_vma=False)
```

time: 311 us -> 242 us (0.78)
  local copies, waits for them, and re-layouts: 63.3 us -> 1.87 us
  matrix products: 101 us -> 49.1 us
  Pallas kernels: 0 us -> 49.2 us
    dot_general x2 -> x0, local copies, waits for them, and re-layouts: 61.9 us -> none  [the longest x1 41 us: attention_layer(): jnp.dot(normed, q_weight, preferred_element_type=jnp.float32)]
    dot_general x6 -> x0, matrix products: 52.4 us -> none  [the longest x1 15.6 us: attention_layer(): jnp.dot(normed, q_weight, preferred_element_type=jnp.float32)]
    pallas_call x0 -> x1, Pallas kernels: none -> 49.2 us  [attention(): pl.pallas_call(functools.partial(attention_kernel, rows), out_shape=(row_...]
where the time goes in v2:
time: 242 us
  waiting for transfers between devices  124 us (51%)
  Pallas kernels  49.2 us (20%)
  matrix products  49.1 us (20%)
  between operations  13.4 us (6%)
  other arithmetic  4.29 us (2%)
    reduce_scatter x1, waiting for transfers between devices, device_fn(): summed = lax.psum_scatter(part_sum, 'dev', scatter_dimension=0, tiled=True)  75.9 us
    pallas_call x1, Pallas kernels, attention(): pl.pallas_call(functools.partial(attention_kernel, rows), out_shape=(row_...  49.2 us
    all_gather x1, waiting for transfers between devices, device_fn(): h_all = lax.all_gather(h_rows, 'dev', axis=0, tiled=True)  48.1 us
    dot_general x1, matrix products, ffn_partial(): return jnp.dot(act_rows, down_weight, preferred_element_type=jnp.float32)  30 us
    dot_general x1, matrix products, ffn_partial(): gate = jnp.dot(h_rows, gate_weight, preferred_element_type=jnp.float32)  19.1 us
  transfers between devices with their start and end apart: 2, of which 2 were waited for; matrix products, arithmetic and copies ran while one was open for 0% of the time, Pallas kernels for 0%

profile of v2, /device:TPU:0, one launch (start us, length us, event | category | flops | bytes accessed | tf_op | source)
XLA Modules:
  0.0 242.0 jit_solution(8388479150012657012)
XLA Ops:
  6.5 0.0 all-gather.2.cloned.1.call-start
  6.6 1.3 fusion.13
  7.8 1.9 constant_dynamic-slice_fusion.x_ref
  9.7 0.2 fusion.12
  9.9 0.7 pad_maximum_fusion
  10.6 49.2 %attention.1 = (bf16[64,4096]{1,0:T(8,128)(2,1)}, bf16[64,4096]{1,0:T(8,128)(2,1)}) custom-call(bf16[64,4096]{1,0:T(8,128)(2,1)} %constant_dynamic-slice_fusion.x_ref, f32[1,4096]{1,0:T(1,128)} %gain_ref.1, f32[1,4096]{1,0:T(1,128)} %ffn_gain_ref.1, f32[64,128]{1,0:T(8,128)} %get-tuple-element.14.cos_ref, f32[64,128]{1,0:T(8,128)} %get-tuple-element.15.sin_ref, ...), custom_call_target="tpu_custom_call" | custom-call | flops 5368709120 | bytes 83886080 | tf_op jit(solution)/shard_map/attention/pallas_call | solution.py:187
  59.8 0.0 all-gather.2.cloned.1.call-update
  59.8 0.0 reduce-scatter.2.cloned.1.call-start
  59.9 48.1 %all-gather.2.cloned.1.call-done = bf16[256,4096]{1,0:T(8,128)(2,1)} async-done(((bf16[64,4096]{1,0:T(8,128)(2,1)}), bf16[256,4096]{1,0:T(8,128)(2,1)}) %all-gather.2.cloned.1.call-update) | async-done | bytes 2097168 | tf_op jit(solution)/shard_map/all_gather | solution.py:249
  108.0 0.0 copy-start.1
  108.0 19.1 %fusion.4 = f32[256,3584]{1,0:T(8,128)} fusion(bf16[256,4096]{1,0:T(8,128)(2,1)} %all-gather.2.cloned.1.call-done, bf16[1,4096,3584]{2,1,0:T(8,128)(2,1)} %param.21), kind=kOutput, calls=%fused_computation.4 | convolution fusion | flops 7516192768 | bytes 35127296 | tf_op jit(solution)/shard_map/dot_general | solution.py:216
  127.1 0.0 copy-done.1
  127.1 30.0 %fusion = f32[256,4096]{1,0:T(8,128)} fusion(bf16[1,3584,4096]{2,1,0:T(8,128)(2,1)} %param.23, bf16[256,4096]{1,0:T(8,128)(2,1)S(1)} %copy-done.1, bf16[1,4096,3584]{2,1,0:T(8,128)(2,1)} %param.22, f32[256,3584]{1,0:T(8,128)} %fusion.4), kind=kOutput, calls=%fused_computation | convolution fusion | flops 15037890560 | bytes 68681728 | tf_op jit(solution)/shard_map/dot_general | solution.py:219
  157.2 0.0 copy-start
  157.2 0.0 reduce-scatter.2.cloned.1.call-update
  157.2 75.9 %reduce-scatter.2.cloned.1.call-done = f32[64,4096]{1,0:T(8,128)} async-done(((f32[256,4096]{1,0:T(8,128)}), f32[64,4096]{1,0:T(8,128)}) %reduce-scatter.2.cloned.1.call-update) | async-done | bytes 1048592 | tf_op jit(solution)/shard_map/reduce_scatter | solution.py:251
  233.0 0.0 copy-done
  233.0 2.1 add_convert_fusion
  (1 shorter events, 0.0 us)
Async XLA Ops:
  6.5 101.5 %all-gather.2.cloned.1.call-start = ((), (), s32[]{:S(2)}) async-start(), calls=%async_computation.1 | async-start | bytes 2621440 | tf_op jit(solution)/shard_map/all_gather | solution.py:249
  59.8 173.2 %reduce-scatter.2.cloned.1.call-start = ((), (), s32[]{:S(2)}) async-start(), calls=%async_computation.2 | async-start | bytes 5242880 | tf_op jit(solution)/shard_map/reduce_scatter | solution.py:251
  108.0 19.1 %copy-start.1 = (bf16[256,4096]{1,0:T(8,128)(2,1)S(1)}, bf16[256,4096]{1,0:T(8,128)(2,1)}, u32[]{:S(2)}) copy-start(bf16[256,4096]{1,0:T(8,128)(2,1)} %all-gather.2.cloned.1.call-done) | copy-start | bytes 6291460
  157.2 75.9 %copy-start = (bf16[64,4096]{1,0:T(8,128)(2,1)S(1)}, bf16[64,4096]{1,0:T(8,128)(2,1)}, u32[]{:S(2)}) copy-start(bf16[64,4096]{1,0:T(8,128)(2,1)} %get-tuple-element.7) | copy-start | bytes 1572868
Sparse Core Ops, SparseCore 0:
  60.0 48.0 all-gather.1
  157.3 75.6 reduce-scatter.1

commit v3 on v2

--- a/solution.py
+++ b/solution.py
@@ -212,11 +212,247 @@
     )(x_rows, gain_attn[None], gain_ffn[None], cos_full, sin_full, lengths, k_cache, v_cache, w_q, w_kv, w_o)
 
 
-def ffn_partial(h_rows, gate_weight, up_weight, down_weight):
-    gate = jnp.dot(h_rows, gate_weight, preferred_element_type=jnp.float32)
-    up_proj = jnp.dot(h_rows, up_weight, preferred_element_type=jnp.float32)
-    act_rows = (jax.nn.silu(gate) * up_proj).astype(jnp.bfloat16)
-    return jnp.dot(act_rows, down_weight, preferred_element_type=jnp.float32)
+FFN_SLOTS = 10
+
+
+def ffn_kernel(h_ref, x1_ref, wg_hbm, wu_hbm, wd_hbm, out_ref, ring, h_all, u_s, part, recv,
+               w_sem, h_send, h_recv, p_send, p_recv):
+    rows, width = h_ref.shape
+    depth = wd_hbm.shape[0]
+    n_ff = depth // TILE
+    n_col = width // TILE
+    per_pass = 2 * n_ff + n_col
+    dev = lax.axis_index('dev')
+    flip = dev >= 2
+    is_end = (dev == 0) | (dev == 3)
+    is_mid = (dev == 1) | (dev == 2)
+    me = jnp.where(is_end, 0, 1)
+    end_dev = jnp.where(flip, 3, 0)
+    mid_dev = jnp.where(flip, 2, 1)
+    far_dev = jnp.where(flip, 1, 2)
+
+    def gate_copy(t, slot):
+        cols = pl.ds(pl.multiple_of(t * TILE, TILE), TILE)
+        return pltpu.make_async_copy(wg_hbm.at[:, cols], ring.at[slot], w_sem.at[slot])
+
+    def up_copy(t, slot):
+        cols = pl.ds(pl.multiple_of(t * TILE, TILE), TILE)
+        return pltpu.make_async_copy(wu_hbm.at[:, cols], ring.at[slot], w_sem.at[slot])
+
+    def down_copy(t, slot):
+        cols = pl.ds(pl.multiple_of(t * TILE, TILE), TILE)
+        return pltpu.make_async_copy(wd_hbm.at[:, cols], ring.at[slot, pl.ds(0, depth)], w_sem.at[slot])
+
+    def start_tile(i):
+        slot = lax.rem(i, FFN_SLOTS)
+        r = lax.rem(i, per_pass)
+        live = i < 2 * per_pass
+
+        @pl.when(live & (r < 2 * n_ff) & (lax.rem(r, 2) == 0))
+        def _():
+            gate_copy(r // 2, slot).start()
+
+        @pl.when(live & (r < 2 * n_ff) & (lax.rem(r, 2) == 1))
+        def _():
+            up_copy(r // 2, slot).start()
+
+        @pl.when(live & (r >= 2 * n_ff))
+        def _():
+            down_copy(r - 2 * n_ff, slot).start()
+
+    def first(i, carry):
+        start_tile(i)
+        return carry
+
+    lax.fori_loop(0, FFN_SLOTS, first, 0)
+
+    def send_h(src, block, k, target):
+        return pltpu.make_async_remote_copy(
+            src_ref=src, dst_ref=h_all.at[block], send_sem=h_send.at[k], recv_sem=h_recv.at[block],
+            device_id={'dev': target}, device_id_type=pl.DeviceIdType.MESH)
+
+    def send_part(j, c, slot, target):
+        return pltpu.make_async_remote_copy(
+            src_ref=part.at[j, c], dst_ref=recv.at[slot, c], send_sem=p_send.at[j, c], recv_sem=p_recv.at[slot, c],
+            device_id={'dev': target}, device_id_type=pl.DeviceIdType.MESH)
+
+    def signal(target):
+        pl.semaphore_signal(pltpu.get_barrier_semaphore(), inc=1, device_id={'dev': target},
+                            device_id_type=pl.DeviceIdType.MESH)
+
+    @pl.when(is_end)
+    def _():
+        signal(mid_dev)
+        pl.semaphore_wait(pltpu.get_barrier_semaphore(), 1)
+        send_h(h_ref, 0, 0, mid_dev).start()
+
+    @pl.when(is_mid)
+    def _():
+        signal(end_dev)
+        signal(far_dev)
+        pl.semaphore_wait(pltpu.get_barrier_semaphore(), 2)
+        send_h(h_ref, 1, 0, end_dev).start()
+        send_h(h_ref, 2, 1, far_dev).start()
+
+    h_all[me] = h_ref[...]
+
+    @pl.when(is_end)
+    def _():
+        send_h(h_ref, 1, 0, mid_dev).wait_recv()
+
+    @pl.when(is_mid)
+    def _():
+        send_h(h_ref, 0, 0, end_dev).wait_recv()
+        send_h(h_all.at[0], 3, 2, far_dev).start()
+        send_h(h_ref, 2, 0, end_dev).wait_recv()
+        send_h(h_all.at[2], 2, 3, end_dev).start()
+
+    for half in range(2):
+        def ff_step(t, carry):
+            i = half * per_pass + 2 * t
+            slot_g, slot_u = lax.rem(i, FFN_SLOTS), lax.rem(i + 1, FFN_SLOTS)
+            h = h_all[2 * half:2 * half + 2].reshape(2 * rows, width)
+            gate_copy(t, slot_g).wait()
+            gate = jnp.dot(h, ring[slot_g], preferred_element_type=jnp.float32)
+            start_tile(i + FFN_SLOTS)
+            up_copy(t, slot_u).wait()
+            up = jnp.dot(h, ring[slot_u], preferred_element_type=jnp.float32)
+            start_tile(i + 1 + FFN_SLOTS)
+            u_s[:, pl.ds(pl.multiple_of(t * TILE, TILE), TILE)] = (jax.nn.silu(gate) * up).astype(jnp.bfloat16)
+            return carry
+
+        def down_step(c, carry):
+            i = half * per_pass + 2 * n_ff + c
+            slot = lax.rem(i, FFN_SLOTS)
+            down_copy(c, slot).wait()
+            y = jnp.dot(u_s[...], ring[slot, :depth], preferred_element_type=jnp.float32)
+            start_tile(i + FFN_SLOTS)
+            part[2 * half, c] = y[:rows]
+            part[2 * half + 1, c] = y[rows:]
+
+            @pl.when(is_end)
+            def _():
+                send_part(2 * half + 1, c, 2 * half, mid_dev).start()
+
+            if half == 0:
+                @pl.when(is_mid & (c == n_col - 3))
+                def _():
+                    send_h(h_ref, 3, 0, end_dev).wait_recv()
+                    send_h(h_all.at[3], 3, 4, end_dev).start()
+
+            return carry
+
+        if half == 1:
+            @pl.when(is_end)
+            def _():
+                send_h(h_ref, 2, 0, mid_dev).wait_recv()
+                send_h(h_ref, 3, 0, mid_dev).wait_recv()
+
+        lax.fori_loop(0, n_ff, ff_step, 0)
+        lax.fori_loop(0, n_col, down_step, 0)
+
+    def finish(c, y):
+        cols = pl.ds(pl.multiple_of(c * TILE, TILE), TILE)
+        y = y.astype(jnp.bfloat16).astype(jnp.float32)
+        out_ref[:, cols] = (x1_ref[:, cols].astype(jnp.float32) + y).astype(jnp.bfloat16)
+
+    @pl.when(is_end)
+    def _():
+        def second(c, carry):
+            send_part(2, c, 1, mid_dev).start()
+            return carry
+
+        def home(c, carry):
+            send_part(0, c, 0, mid_dev).wait_recv()
+            finish(c, part[0, c] + recv[0, c])
+            return carry
+
+        def drain(c, carry):
+            for j in (1, 3, 2):
+                send_part(j, c, 0, mid_dev).wait_send()
+            return carry
+
+        lax.fori_loop(0, n_col, second, 0)
+        lax.fori_loop(0, n_col, home, 0)
+        lax.fori_loop(0, n_col, drain, 0)
+        send_h(h_ref, 0, 0, mid_dev).wait_send()
+
+    @pl.when(is_mid)
+    def _():
+        def back(c):
+            send_part(0, c, 4, far_dev).wait_recv()
+            part[0, c] += recv[4, c]
+            send_part(0, c, 0, end_dev).start()
+
+        def across(c, carry):
+            send_part(3, c, 2, end_dev).wait_recv()
+            part[3, c] += recv[2, c]
+            send_part(3, c, 4, far_dev).start()
+
+            @pl.when(c > 0)
+            def _():
+                back(c - 1)
+
+            return carry
+
+        def home(c):
+            send_part(1, c, 0, end_dev).wait_recv()
+            send_part(1, c, 3, far_dev).wait_recv()
+            finish(c, part[1, c] + recv[0, c] + recv[3, c])
+
+        def near(c, carry):
+            send_part(2, c, 1, end_dev).wait_recv()
+            part[2, c] += recv[1, c]
+            send_part(2, c, 3, far_dev).start()
+
+            @pl.when(c > 0)
+            def _():
+                home(c - 1)
+
+            return carry
+
+        def drain(c, carry):
+            for j in (3, 0, 2):
+                send_part(j, c, 0, far_dev).wait_send()
+            return carry
+
+        lax.fori_loop(0, n_col, across, 0)
+        back(n_col - 1)
+        lax.fori_loop(0, n_col, near, 0)
+        home(n_col - 1)
+        lax.fori_loop(0, n_col, drain, 0)
+        for k in range(5):
+            send_h(h_ref, 0, k, end_dev).wait_send()
+
+
+def ffn(h_rows, x_mid, w_gate, w_up, w_down):
+    rows, width = h_rows.shape
+    depth = w_down.shape[0]
+    n_col = width // TILE
+    vmem = pl.BlockSpec(memory_space=pltpu.VMEM)
+    hbm = pl.BlockSpec(memory_space=pl.ANY)
+    weights = 3 * w_gate.size
+    return pl.pallas_call(
+        ffn_kernel,
+        out_shape=jax.ShapeDtypeStruct((rows, width), jnp.bfloat16),
+        in_specs=[vmem, vmem, hbm, hbm, hbm],
+        out_specs=vmem,
+        scratch_shapes=[
+            pltpu.VMEM((FFN_SLOTS, width, TILE), jnp.bfloat16),
+            pltpu.VMEM((4, rows, width), jnp.bfloat16),
+            pltpu.VMEM((2 * rows, depth), jnp.bfloat16),
+            pltpu.VMEM((4, n_col, rows, TILE), jnp.float32),
+            pltpu.VMEM((5, n_col, rows, TILE), jnp.float32),
+            pltpu.SemaphoreType.DMA((FFN_SLOTS,)),
+            pltpu.SemaphoreType.DMA((5,)),
+            pltpu.SemaphoreType.DMA((4,)),
+            pltpu.SemaphoreType.DMA((4, n_col)),
+            pltpu.SemaphoreType.DMA((5, n_col)),
+        ],
+        compiler_params=pltpu.CompilerParams(vmem_limit_bytes=VMEM_LIMIT, collective_id=0, has_side_effects=True),
+        cost_estimate=pl.CostEstimate(flops=8 * rows * weights, bytes_accessed=4 * weights, transcendentals=0),
+        name="ffn",
+    )(h_rows, x_mid, w_gate, w_up, w_down)
 
 
 def own_rows(local, side_idx, n_side):
@@ -246,10 +482,7 @@
         for layer in range(w_q.shape[0]):
             x_mid, h_rows = attention(x_rows, lengths, k_cache[layer], v_cache[layer], w_q[layer], w_kv[layer], w_o[layer],
                                       attn_gain[layer], ffn_gain[layer])
-            h_all = lax.all_gather(h_rows, 'dev', axis=0, tiled=True)
-            part_sum = ffn_partial(h_all, w_gate[layer], w_up[layer], w_down[layer])
-            summed = lax.psum_scatter(part_sum, 'dev', scatter_dimension=0, tiled=True)
-            x_rows = (x_mid.astype(jnp.float32) + summed.astype(jnp.bfloat16).astype(jnp.float32)).astype(jnp.bfloat16)
+            x_rows = ffn(h_rows, x_mid, w_gate[layer], w_up[layer], w_down[layer])
         return x_rows
 
     return jax.shard_map(device_fn, mesh=mesh, in_specs=in_specs, out_specs=out_specs, check_vma=False)

time: 242 us -> 163 us (0.67)
  the two profiles are of different devices: /device:TPU:0 before, /device:TPU:12 now
where the time goes in v3:
time: 163 us
  Pallas kernels  157 us (96%)
  local copies, waits for them, and re-layouts  3.74 us (2%)
  other arithmetic  2.24 us (1%)
    pallas_call x1, Pallas kernels, ffn(): pl.pallas_call(ffn_kernel, out_shape=jax.ShapeDtypeStruct((rows, width),...  108 us
    pallas_call x1, Pallas kernels, attention(): pl.pallas_call(functools.partial(attention_kernel, rows), out_shape=(row_...  49.2 us

profile of v3, /device:TPU:12, one launch (start us, length us, event | category | flops | bytes accessed | tf_op | source)
XLA Modules:
  0.0 162.7 jit_solution(8197343041684083073)
XLA Ops:
  0.0 1.3 fusion.1
  1.3 0.2 fusion
  1.5 0.7 pad_maximum_fusion
  2.2 1.9 %constant_dynamic-slice_fusion.x_ref = bf16[64,4096]{1,0:T(8,128)(2,1)} fusion(bf16[256,4096]{1,0:T(8,128)(2,1)} %param.12, s32[]{:T(128)S(6)} %select_n.4), kind=kLoop, calls=%fused_computation.6 | loop fusion | bytes 1048580 | tf_op jit(solution)/shard_map/dynamic_slice | solution.py:460
  4.1 49.2 %attention.1 = (bf16[64,4096]{1,0:T(8,128)(2,1)}, bf16[64,4096]{1,0:T(8,128)(2,1)}) custom-call(bf16[64,4096]{1,0:T(8,128)(2,1)} %constant_dynamic-slice_fusion.x_ref, f32[1,4096]{1,0:T(1,128)} %gain_ref.1, f32[1,4096]{1,0:T(1,128)} %ffn_gain_ref.1, f32[64,128]{1,0:T(8,128)} %get-tuple-element.14.cos_ref, f32[64,128]{1,0:T(8,128)} %get-tuple-element.15.sin_ref, ...), custom_call_target="tpu_custom_call" | custom-call | flops 5368709120 | bytes 83886080 | tf_op jit(solution)/shard_map/attention/pallas_call | solution.py:187
  53.3 107.6 %ffn.1 = bf16[64,4096]{1,0:T(8,128)(2,1)} custom-call(bf16[64,4096]{1,0:T(8,128)(2,1)} %get-tuple-element.7.h_ref, bf16[64,4096]{1,0:T(8,128)(2,1)} %get-tuple-element.8.x1_ref, bf16[4096,3584]{1,0:T(8,128)(2,1)} %bitcast.12, bf16[4096,3584]{1,0:T(8,128)(2,1)} %bitcast.13, bf16[3584,4096]{1,0:T(8,128)(2,1)} %bitcast.14), custom_call_target="tpu_custom_call" | custom-call | flops 22548578304 | bytes 176160768 | tf_op jit(solution)/shard_map/ffn/pallas_call | solution.py:435
  160.9 1.9 %copy.14 = bf16[64,4096]{1,0:T(8,128)(2,1)} copy(bf16[64,4096]{1,0:T(8,128)(2,1)} %ffn.1) | data formatting | bytes 1048576
  (1 shorter events, 0.0 us)

commit v4 on v1

v4 whole, which is shorter than its diff:
```python
import functools

import jax
import jax.numpy as jnp
import numpy as np
from jax import lax
from jax.experimental import pallas as pl
from jax.experimental.pallas import tpu as pltpu
from jax.sharding import PartitionSpec as P

EPS = 1e-5
ROPE_BASE = 10000.0
TILE = 512
SLOTS = 8
SEQS = 16
KV_BUFS = 4
VMEM_LIMIT = 66_000_000
MESH = pl.DeviceIdType.MESH


def rope_tables(cache, head):
    half = head // 2
    freqs = np.power(np.float32(ROPE_BASE), -np.arange(half, dtype=np.float32) / np.float32(half))
    angle = np.arange(cache + 1, dtype=np.float32)[:, None] * freqs.astype(np.float32)
    cos_part, sin_part = np.cos(angle.astype(np.float64)), np.sin(angle.astype(np.float64))
    cos_full = np.concatenate([cos_part, cos_part], axis=-1).astype(np.float32)
    sin_full = np.concatenate([-sin_part, sin_part], axis=-1).astype(np.float32)
    return cos_full[:, None], sin_full[:, None]


def layer_kernel(rows, len_ref, cos_tab, sin_tab, gain_ref, ffn_gain_ref, x_hbm, k_hbm, v_hbm, wq_hbm, wkv_hbm, wo_hbm,
                 wg_hbm, wu_hbm, wd_hbm, out_ref, ring, kv_buf, x_s, a_s, cos_s, sin_s, q_s, kv_s, ob_s, s_s, p_s,
                 tq, tx, tb, take_s, x1_s, h_all, u_s, part, recv, x_sem, w_sem, kv_sem, give_sem, take_sem,
                 h_send, h_recv, p_send, p_recv):
    width = x_hbm.shape[1]
    _, kv_heads, cache, head = k_hbm.shape
    kv_heads //= 2
    q_cols = wq_hbm.shape[1] // 2
    heads = q_cols // head
    group = heads // kv_heads
    pair = 2 * rows
    n_groups = pair // SEQS
    depth = wd_hbm.shape[0]
    n_q = q_cols // TILE
    n_col = width // TILE
    n_ff = depth // TILE
    o_first = n_q + 2
    ff_first = o_first + n_col
    per_pass = 2 * n_ff + n_col
    n_tiles = ff_first + 2 * per_pass

    side = lax.axis_index('side')
    core = lax.rem(side, 2)
    partner = side + 1 - 2 * core
    base = (side // 2) * pair
    dev = lax.axis_index('dev')
    flip = dev >= 2
    is_end = (dev == 0) | (dev == 3)
    is_mid = (dev == 1) | (dev == 2)
    end_dev = jnp.where(flip, 3, 0)
    mid_dev = jnp.where(flip, 2, 1)
    far_dev = jnp.where(flip, 1, 2)

    def column_copy(hbm, first_row, n_rows, first_col, slot):
        cols = pl.ds(pl.multiple_of(first_col, TILE), TILE)
        return pltpu.make_async_copy(hbm.at[pl.ds(first_row, n_rows), cols], ring.at[slot, pl.ds(0, n_rows)],
                                     w_sem.at[slot])

    def q_copy(t, slot):
        return column_copy(wq_hbm, 0, width, core * q_cols + t * TILE, slot)

    def kv_copy(which, slot):
        return column_copy(wkv_hbm, 0, width, (2 * which + core) * TILE, slot)

    def o_copy(t, slot):
        return column_copy(wo_hbm, core * q_cols, q_cols, t * TILE, slot)

    def gate_copy(t, slot):
        return column_copy(wg_hbm, 0, width, t * TILE, slot)

    def up_copy(t, slot):
        return column_copy(wu_hbm, 0, width, t * TILE, slot)

    def down_copy(t, slot):
        return column_copy(wd_hbm, 0, depth, t * TILE, slot)

    def start_ff(i):
        slot = lax.rem(i, SLOTS)
        r = lax.rem(i - ff_first, per_pass)
        live = i < n_tiles

        @pl.when(live & (r < 2 * n_ff) & (lax.rem(r, 2) == 0))
        def _():
            gate_copy(r // 2, slot).start()

        @pl.when(live & (r < 2 * n_ff) & (lax.rem(r, 2) == 1))
        def _():
            up_copy(r // 2, slot).start()

        @pl.when(live & (r >= 2 * n_ff))
        def _():
            down_copy(r - 2 * n_ff, slot).start()

    def each_kv(i, act):
        buf = lax.rem(i, KV_BUFS)
        at = (pl.ds(base + lax.rem(i, n_groups) * SEQS, SEQS), pl.ds(core * kv_heads, kv_heads))

        @pl.when(i < n_groups)
        def _():
            act(pltpu.make_async_copy(k_hbm.at[at], kv_buf.at[buf], kv_sem.at[buf]))

        @pl.when((i >= n_groups) & (i < 2 * n_groups))
        def _():
            act(pltpu.make_async_copy(v_hbm.at[at], kv_buf.at[buf], kv_sem.at[buf]))

    def start_kv(i):
        each_kv(i, lambda copy: copy.start())

    def wait_kv(i):
        each_kv(i, lambda copy: copy.wait())

    x_copy = pltpu.make_async_copy(x_hbm.at[pl.ds(base, pair)], x_s, x_sem)
    x_copy.start()
    for t in range(n_q):
        q_copy(t, t).start()
    for which in range(2):
        kv_copy(which, n_q + which).start()
    for i in range(KV_BUFS):
        start_kv(i)
    for t in range(SLOTS - o_first):
        o_copy(t, o_first + t).start()

    def signal(target):
        pl.semaphore_signal(pltpu.get_barrier_semaphore(), inc=1, device_id=target, device_id_type=MESH)

    signal({'side': partner})

    @pl.when(is_end)
    def _():
        signal({'dev': mid_dev})
        pl.semaphore_wait(pltpu.get_barrier_semaphore(), 2)

    @pl.when(is_mid)
    def _():
        signal({'dev': end_dev})
        signal({'dev': far_dev})
        pl.semaphore_wait(pltpu.get_barrier_semaphore(), 3)


    def lookup(i, carry):
        n = len_ref[base + i]
        cos_s[pl.ds(i, 1), :] = cos_tab[n]
        sin_s[pl.ds(i, 1), :] = sin_tab[n]
        return carry

    lax.fori_loop(0, pair, lookup, 0)
    x_copy.wait()
    x_f = x_s[...].astype(jnp.float32)
    inv = lax.rsqrt(jnp.mean(x_f * x_f, axis=-1, keepdims=True) + EPS)
    a_s[...] = (x_f * inv * gain_ref[...]).astype(jnp.bfloat16)

    def rotated(tile, i):
        vec = tile[:, i * head:(i + 1) * head]
        return vec * cos_s[...] + pltpu.roll(vec, head // 2, 1) * sin_s[...]

    def q_step(t, carry):
        q_copy(t, t).wait()
        tile = jnp.dot(a_s[...], ring[t], preferred_element_type=jnp.float32)
        for i in range(TILE // head):
            q_s[:, pl.ds(pl.multiple_of(t * TILE + i * head, head), head)] = rotated(tile, i)
        o_copy(t + SLOTS - o_first, t).start()
        return carry

    lax.fori_loop(0, n_q, q_step, 0)
    kv_copy(0, n_q).wait()
    tile = jnp.dot(a_s[...], ring[n_q], preferred_element_type=jnp.float32)
    for i in range(TILE // head):
        kv_s[:, i * head:(i + 1) * head] = rotated(tile, i)
    o_copy(n_col - 2, n_q).start()
    kv_copy(1, n_q + 1).wait()
    kv_s[:, TILE:] = jnp.dot(a_s[...], ring[n_q + 1], preferred_element_type=jnp.float32)
    o_copy(n_col - 1, n_q + 1).start()

    scale = head ** -0.5
    keys = kv_heads * cache
    row_head = lax.broadcasted_iota(jnp.int32, (heads, keys), 0) // group
    col = lax.broadcasted_iota(jnp.int32, (heads, keys), 1)
    key_pos = jnp.where(col // cache == row_head, col % cache, cache + 1)
    nt = (((1,), (1,)), ((), ()))

    def seq_rows(i):
        return pl.ds(pl.multiple_of(i * heads, heads), heads)

    def group_rows(g):
        return pl.ds(pl.multiple_of(g * SEQS, SEQS), SEQS)

    def spread_heads(g, first_col):
        for h in range(heads):
            at = first_col + (h // group) * head
            tx[pl.ds(h, SEQS, stride=heads), :] = kv_s[group_rows(g), at:at + head]
        return tx[...].astype(jnp.bfloat16).astype(jnp.float32)

    def score_group(g, carry):
        buf = lax.rem(g, KV_BUFS)
        for h in range(heads):
            tq[pl.ds(h, SEQS, stride=heads), :] = q_s[group_rows(g), h * head:(h + 1) * head]
        q = tq[...].astype(jnp.bfloat16)
        tb[...] = q
        s_own = jnp.sum(q.astype(jnp.float32) * spread_heads(g, 0), axis=-1, keepdims=True) * scale
        s_s[g, :, keys:] = jnp.broadcast_to(s_own, (SEQS * heads, head))
        wait_kv(g)

        def one(i, carry):
            k = kv_buf[buf, i].reshape(keys, head)
            s_s[g, seq_rows(i), :keys] = lax.dot_general(tb[seq_rows(i), :], k, nt, preferred_element_type=jnp.float32)
            return carry

        lax.fori_loop(0, SEQS, one, 0, unroll=True)
        start_kv(g + KV_BUFS)
        return carry

    def softmax_group(g, carry):
        def one(i, carry):
            n = len_ref[base + g * SEQS + i]
            s = jnp.where(key_pos < n, s_s[g, seq_rows(i), :keys] * scale, -1e30)
            s_own = s_s[g, seq_rows(i), keys:]
            top = jnp.maximum(jnp.max(s, axis=-1, keepdims=True), s_own)
            e = jnp.exp(s - top[:, :1])
            e_own = jnp.exp(s_own - top)
            p_s[g, seq_rows(i), :] = e.astype(jnp.bfloat16)
            s_s[g, seq_rows(i), :head] = jnp.sum(e, axis=-1, keepdims=True) + e_own
            s_s[g, seq_rows(i), keys:] = e_own.astype(jnp.bfloat16).astype(jnp.float32)
            return carry

        lax.fori_loop(0, SEQS, one, 0, unroll=True)
        return carry

    def mix_group(g, carry):
        buf = lax.rem(n_groups + g, KV_BUFS)
        wait_kv(n_groups + g)

        def one(i, carry):
            v = kv_buf[buf, i].reshape(keys, head)
            tq[seq_rows(i), :] = jnp.dot(p_s[g, seq_rows(i), :], v, preferred_element_type=jnp.float32)
            return carry

        lax.fori_loop(0, SEQS, one, 0, unroll=True)
        start_kv(n_groups + g + KV_BUFS)
        tq[...] = (tq[...] + s_s[g, :, keys:] * spread_heads(g, TILE)) / s_s[g, :, :head]
        for h in range(heads):
            q_s[group_rows(g), h * head:(h + 1) * head] = tq[pl.ds(h, SEQS, stride=heads), :]
        return carry

    lax.fori_loop(0, n_groups, score_group, 0)
    lax.fori_loop(0, n_groups, softmax_group, 0)
    lax.fori_loop(0, n_groups, mix_group, 0)
    ob_s[...] = q_s[...].astype(jnp.bfloat16)

    def give(t):
        return pltpu.make_async_remote_copy(
            src_ref=part.at[1, t], dst_ref=take_s.at[t], send_sem=give_sem.at[t], recv_sem=take_sem.at[t],
            device_id={'side': partner}, device_id_type=MESH)

    def o_step(t, carry):
        slot = lax.rem(o_first + t, SLOTS)
        o_copy(t, slot).wait()
        y = jnp.dot(ob_s[...], ring[slot, :q_cols], preferred_element_type=jnp.float32)
        part[1, t] = jnp.where(core == 0, y[rows:], y[:rows])
        give(t).start()
        part[0, t] = jnp.where(core == 0, y[:rows], y[rows:])
        start_ff(ff_first - o_first + o_first + t)
        return carry

    lax.fori_loop(0, n_col, o_step, 0)
    own_rows = pl.ds(pl.multiple_of(core * rows, rows), rows)

    def x1_step(t, square):
        give(t).wait_recv()
        give(t).wait_send()
        cols = pl.ds(pl.multiple_of(t * TILE, TILE), TILE)
        x1 = (x_s[own_rows, cols].astype(jnp.float32) + (part[0, t] + take_s[t])).astype(jnp.bfloat16)
        x1_s[:, cols] = x1
        x1_f = x1.astype(jnp.float32)
        return square + jnp.sum(x1_f * x1_f, axis=-1, keepdims=True)

    square = lax.fori_loop(0, n_col, x1_step, jnp.zeros((rows, 1), jnp.float32))
    inv = lax.rsqrt(square / width + EPS)
    me = jnp.where(is_end, 0, 1)
    h_all[me] = (x1_s[...].astype(jnp.float32) * inv * ffn_gain_ref[...]).astype(jnp.bfloat16)

    def send_h(src, dst, k, target):
        return pltpu.make_async_remote_copy(
            src_ref=h_all.at[src], dst_ref=h_all.at[dst], send_sem=h_send.at[k], recv_sem=h_recv.at[dst],
            device_id={'dev': target}, device_id_type=MESH)

    def send_part(j, c, slot, target):
        return pltpu.make_async_remote_copy(
            src_ref=part.at[j, c], dst_ref=recv.at[slot, c], send_sem=p_send.at[j, c], recv_sem=p_recv.at[slot, c],
            device_id={'dev': target}, device_id_type=MESH)

    @pl.when(is_end)
    def _():
        send_h(0, 0, 0, mid_dev).start()
        send_h(0, 1, 0, mid_dev).wait_recv()

    @pl.when(is_mid)
    def _():
        send_h(1, 1, 0, end_dev).start()
        send_h(1, 2, 1, far_dev).start()
        send_h(1, 0, 0, end_dev).wait_recv()
        send_h(0, 3, 2, far_dev).start()
        send_h(1, 2, 0, end_dev).wait_recv()
        send_h(2, 2, 3, end_dev).start()

    for half in range(2):
        def ff_step(t, carry):
            i = ff_first + half * per_pass + 2 * t
            slot_g, slot_u = lax.rem(i, SLOTS), lax.rem(i + 1, SLOTS)
            h = h_all[2 * half:2 * half + 2].reshape(2 * rows, width)
            gate_copy(t, slot_g).wait()
            gate = jnp.dot(h, ring[slot_g], preferred_element_type=jnp.float32)
            start_ff(i + SLOTS)
            up_copy(t, slot_u).wait()
            up = jnp.dot(h, ring[slot_u], preferred_element_type=jnp.float32)
            start_ff(i + 1 + SLOTS)
            u_s[:, pl.ds(pl.multiple_of(t * TILE, TILE), TILE)] = (jax.nn.silu(gate) * up).astype(jnp.bfloat16)
            return carry

        def down_step(c, carry):
            i = ff_first + half * per_pass + 2 * n_ff + c
            slot = lax.rem(i, SLOTS)
            down_copy(c, slot).wait()
            y = jnp.dot(u_s[...], ring[slot, :depth], preferred_element_type=jnp.float32)
            start_ff(i + SLOTS)
            part[2 * half, c] = y[:rows]
            part[2 * half + 1, c] = y[rows:]

            @pl.when(is_end)
            def _():
                send_part(2 * half + 1, c, 2 * half, mid_dev).start()

            if half == 0:
                @pl.when(is_mid & (c == n_col - 3))
                def _():
                    send_h(1, 3, 0, end_dev).wait_recv()
                    send_h(3, 3, 4, end_dev).start()

            return carry

        if half == 1:
            @pl.when(is_end)
            def _():
                send_h(0, 2, 0, mid_dev).wait_recv()
                send_h(0, 3, 0, mid_dev).wait_recv()

        lax.fori_loop(0, n_ff, ff_step, 0)
        lax.fori_loop(0, n_col, down_step, 0)

    def finish(c, y):
        cols = pl.ds(pl.multiple_of(c * TILE, TILE), TILE)
        y = y.astype(jnp.bfloat16).astype(jnp.float32)
        out_ref[:, cols] = (x1_s[:, cols].astype(jnp.float32) + y).astype(jnp.bfloat16)

    @pl.when(is_end)
    def _():
        def second(c, carry):
            send_part(2, c, 1, mid_dev).start()
            return carry

        def home(c, carry):
            send_part(0, c, 0, mid_dev).wait_recv()
            finish(c, part[0, c] + recv[0, c])
            return carry

        def drain(c, carry):
            for j in (1, 3, 2):
                send_part(j, c, 0, mid_dev).wait_send()
            return carry

        lax.fori_loop(0, n_col, second, 0)
        lax.fori_loop(0, n_col, home, 0)
        lax.fori_loop(0, n_col, drain, 0)
        send_h(0, 0, 0, mid_dev).wait_send()

    @pl.when(is_mid)
    def _():
        def back(c):
            send_part(0, c, 4, far_dev).wait_recv()
            part[0, c] += recv[4, c]
            send_part(0, c, 0, end_dev).start()

        def across(c, carry):
            send_part(3, c, 2, end_dev).wait_recv()
            part[3, c] += recv[2, c]
            send_part(3, c, 4, far_dev).start()

            @pl.when(c > 0)
            def _():
                back(c - 1)

            return carry

        def home(c):
            send_part(1, c, 0, end_dev).wait_recv()
            send_part(1, c, 3, far_dev).wait_recv()
            finish(c, part[1, c] + recv[0, c] + recv[3, c])

        def near(c, carry):
            send_part(2, c, 1, end_dev).wait_recv()
            part[2, c] += recv[1, c]
            send_part(2, c, 3, far_dev).start()

            @pl.when(c > 0)
            def _():
                home(c - 1)

            return carry

        def drain(c, carry):
            for j in (3, 0, 2):
                send_part(j, c, 0, far_dev).wait_send()
            return carry

        lax.fori_loop(0, n_col, across, 0)
        back(n_col - 1)
        lax.fori_loop(0, n_col, near, 0)
        home(n_col - 1)
        lax.fori_loop(0, n_col, drain, 0)
        for k in range(5):
            send_h(0, 0, k, end_dev).wait_send()


def layer_step(hidden, lengths, k_cache, v_cache, w_q, w_kv, w_o, gain_attn, gain_ffn, w_gate, w_up, w_down, n_side):
    rows, width = hidden.shape[0] // n_side, hidden.shape[1]
    _, kv_heads, cache, head = k_cache.shape
    q_cols = w_q.shape[1] // 2
    heads = q_cols // head
    depth = w_down.shape[0]
    n_col = width // TILE
    assert kv_heads * head == 2 * TILE, "tile"
    cos_tab, sin_tab = rope_tables(cache, head)
    vmem = pl.BlockSpec(memory_space=pltpu.VMEM)
    hbm = pl.BlockSpec(memory_space=pl.ANY)
    f32, bf16 = jnp.float32, jnp.bfloat16
    dma = pltpu.SemaphoreType.DMA
    kv_block = (KV_BUFS, SEQS, kv_heads // 2, cache, head)
    return pl.pallas_call(
        functools.partial(layer_kernel, rows),
        out_shape=jax.ShapeDtypeStruct((rows, width), bf16),
        in_specs=[pl.BlockSpec(memory_space=pltpu.SMEM)] + [vmem] * 4 + [hbm] * 9,
        out_specs=vmem,
        scratch_shapes=[
            pltpu.VMEM((SLOTS, width, TILE), bf16),
            pltpu.VMEM(kv_block, bf16),
            pltpu.VMEM((2 * rows, width), bf16),
            pltpu.VMEM((2 * rows, width), bf16),
            pltpu.VMEM((2 * rows, head), f32),
            pltpu.VMEM((2 * rows, head), f32),
            pltpu.VMEM((2 * rows, q_cols), f32),
            pltpu.VMEM((2 * rows, 2 * TILE), f32),
            pltpu.VMEM((2 * rows, q_cols), bf16),
            pltpu.VMEM((2 * rows // SEQS, SEQS * heads, kv_heads // 2 * cache + head), f32),
            pltpu.VMEM((2 * rows // SEQS, SEQS * heads, kv_heads // 2 * cache), bf16),
            pltpu.VMEM((SEQS * heads, head), f32),
            pltpu.VMEM((SEQS * heads, head), f32),
            pltpu.VMEM((SEQS * heads, head), bf16),
            pltpu.VMEM((n_col, rows, TILE), f32),
            pltpu.VMEM((rows, width), bf16),
            pltpu.VMEM((4, rows, width), bf16),
            pltpu.VMEM((2 * rows, depth), bf16),
            pltpu.VMEM((4, n_col, rows, TILE), f32),
            pltpu.VMEM((5, n_col, rows, TILE), f32),
            dma(()),
            dma((SLOTS,)),
            dma((KV_BUFS,)),
            dma((n_col,)),
            dma((n_col,)),
            dma((5,)),
            dma((4,)),
            dma((4, n_col)),
            dma((5, n_col)),
        ],
        compiler_params=pltpu.CompilerParams(vmem_limit_bytes=VMEM_LIMIT, collective_id=0, has_side_effects=True),
        name="layer",
    )(lengths, jnp.asarray(cos_tab), jnp.asarray(sin_tab), gain_attn[None], gain_ffn[None], hidden, k_cache, v_cache,
      w_q, w_kv, w_o, w_gate, w_up, w_down)


def solution(mesh):
    n_side = mesh.shape['side']
    assert n_side == 4 and mesh.shape['dev'] == 4, "mesh"
    batch_axes = ('inst', 'dev')
    in_specs = (
        P(batch_axes, None),
        P(batch_axes),
        P(None, batch_axes, None, None, None),
        P(None, batch_axes, None, None, None),
        P(), P(), P(), P(), P(),
        P(None, None, 'dev'),
        P(None, None, 'dev'),
        P(None, 'dev', None),
    )
    out_specs = P(('inst', 'dev', 'side'), None)

    def device_fn(hidden, cache_len, k_cache, v_cache, w_q, w_kv, w_o, attn_gain, ffn_gain, w_gate, w_up, w_down):
        assert w_q.shape[0] == 1, "layers"
        return layer_step(hidden, cache_len, k_cache[0], v_cache[0], w_q[0], w_kv[0], w_o[0], attn_gain[0], ffn_gain[0],
                          w_gate[0], w_up[0], w_down[0], n_side)

    return jax.shard_map(device_fn, mesh=mesh, in_specs=in_specs, out_specs=out_specs, check_vma=False)
```

time: 311 us -> 151 us (0.49)
  the two profiles are of different devices: /device:TPU:0 before, /device:TPU:14 now
where the time goes in v4:
time: 151 us
  Pallas kernels  149 us (99%)
  local copies, waits for them, and re-layouts  1.87 us (1%)
    pallas_call x1, Pallas kernels, layer_step(): pl.pallas_call(functools.partial(layer_kernel, rows), out_shape=jax.Shape...  149 us

profile of v4, /device:TPU:14, one launch (start us, length us, event | category | flops | bytes accessed | tf_op | source)
XLA Modules:
  0.0 151.2 jit_solution(8248074935778325323)
XLA Ops:
  0.0 149.3 %layer.1 = bf16[64,4096]{1,0:T(8,128)(2,1)} custom-call(s32[256]{0:T(256)} %len_ref.1, f32[65,1,128]{2,1,0:T(1,128)} %constant.4.clone.cos_tab, f32[65,1,128]{2,1,0:T(1,128)} %constant.5.clone.sin_tab, f32[1,4096]{1,0:T(1,128)} %gain_ref.1, f32[1,4096]{1,0:T(1,128)} %ffn_gain_ref.1, bf16[256,4096]{1,0:T(8,128)(2,1)} %x_hbm.1, ...), custom_call_target="tpu_custom_call" | custom-call | tf_op jit(solution)/shard_map/layer/pallas_call | solution.py:447
  149.4 1.9 %copy.16 = bf16[64,4096]{1,0:T(8,128)(2,1)} copy(bf16[64,4096]{1,0:T(8,128)(2,1)} %layer.1) | data formatting | bytes 1048576

commit v5 on v4

--- a/solution.py
+++ b/solution.py
@@ -13,7 +13,8 @@
 TILE = 512
 SLOTS = 8
 SEQS = 16
-KV_BUFS = 4
+KV_BUFS = 12
+FFN_SLOTS = 10
 VMEM_LIMIT = 66_000_000
 MESH = pl.DeviceIdType.MESH
 
@@ -28,10 +29,9 @@
     return cos_full[:, None], sin_full[:, None]
 
 
-def layer_kernel(rows, len_ref, cos_tab, sin_tab, gain_ref, ffn_gain_ref, x_hbm, k_hbm, v_hbm, wq_hbm, wkv_hbm, wo_hbm,
-                 wg_hbm, wu_hbm, wd_hbm, out_ref, ring, kv_buf, x_s, a_s, cos_s, sin_s, q_s, kv_s, ob_s, s_s, p_s,
-                 tq, tx, tb, take_s, x1_s, h_all, u_s, part, recv, x_sem, w_sem, kv_sem, give_sem, take_sem,
-                 h_send, h_recv, p_send, p_recv):
+def attention_kernel(rows, len_ref, cos_tab, sin_tab, gain_ref, x_hbm, k_hbm, v_hbm, wq_hbm, wkv_hbm, wo_hbm, own_ref,
+                     give_ref, ring, kv_buf, x_s, a_s, cos_s, sin_s, q_s, kv_s, ob_s, s_s, p_s, tq, tx, tb, x_sem, w_sem,
+                     kv_sem):
     width = x_hbm.shape[1]
     _, kv_heads, cache, head = k_hbm.shape
     kv_heads //= 2
@@ -40,26 +40,13 @@
     group = heads // kv_heads
     pair = 2 * rows
     n_groups = pair // SEQS
-    depth = wd_hbm.shape[0]
     n_q = q_cols // TILE
     n_col = width // TILE
-    n_ff = depth // TILE
     o_first = n_q + 2
-    ff_first = o_first + n_col
-    per_pass = 2 * n_ff + n_col
-    n_tiles = ff_first + 2 * per_pass
 
     side = lax.axis_index('side')
     core = lax.rem(side, 2)
-    partner = side + 1 - 2 * core
     base = (side // 2) * pair
-    dev = lax.axis_index('dev')
-    flip = dev >= 2
-    is_end = (dev == 0) | (dev == 3)
-    is_mid = (dev == 1) | (dev == 2)
-    end_dev = jnp.where(flip, 3, 0)
-    mid_dev = jnp.where(flip, 2, 1)
-    far_dev = jnp.where(flip, 1, 2)
 
     def column_copy(hbm, first_row, n_rows, first_col, slot):
         cols = pl.ds(pl.multiple_of(first_col, TILE), TILE)
@@ -74,32 +61,6 @@
 
     def o_copy(t, slot):
         return column_copy(wo_hbm, core * q_cols, q_cols, t * TILE, slot)
-
-    def gate_copy(t, slot):
-        return column_copy(wg_hbm, 0, width, t * TILE, slot)
-
-    def up_copy(t, slot):
-        return column_copy(wu_hbm, 0, width, t * TILE, slot)
-
-    def down_copy(t, slot):
-        return column_copy(wd_hbm, 0, depth, t * TILE, slot)
-
-    def start_ff(i):
-        slot = lax.rem(i, SLOTS)
-        r = lax.rem(i - ff_first, per_pass)
-        live = i < n_tiles
-
-        @pl.when(live & (r < 2 * n_ff) & (lax.rem(r, 2) == 0))
-        def _():
-            gate_copy(r // 2, slot).start()
-
-        @pl.when(live & (r < 2 * n_ff) & (lax.rem(r, 2) == 1))
-        def _():
-            up_copy(r // 2, slot).start()
-
-        @pl.when(live & (r >= 2 * n_ff))
-        def _():
-            down_copy(r - 2 * n_ff, slot).start()
 
     def each_kv(i, act):
         buf = lax.rem(i, KV_BUFS)
@@ -130,30 +91,13 @@
     for t in range(SLOTS - o_first):
         o_copy(t, o_first + t).start()
 
-    def signal(target):
-        pl.semaphore_signal(pltpu.get_barrier_semaphore(), inc=1, device_id=target, device_id_type=MESH)
-
-    signal({'side': partner})
-
-    @pl.when(is_end)
-    def _():
-        signal({'dev': mid_dev})
-        pl.semaphore_wait(pltpu.get_barrier_semaphore(), 2)
-
-    @pl.when(is_mid)
-    def _():
-        signal({'dev': end_dev})
-        signal({'dev': far_dev})
-        pl.semaphore_wait(pltpu.get_barrier_semaphore(), 3)
-
-
     def lookup(i, carry):
         n = len_ref[base + i]
         cos_s[pl.ds(i, 1), :] = cos_tab[n]
         sin_s[pl.ds(i, 1), :] = sin_tab[n]
         return carry
 
-    lax.fori_loop(0, pair, lookup, 0)
+    lax.fori_loop(0, pair, lookup, 0, unroll=8)
     x_copy.wait()
     x_f = x_s[...].astype(jnp.float32)
     inv = lax.rsqrt(jnp.mean(x_f * x_f, axis=-1, keepdims=True) + EPS)
@@ -256,29 +200,109 @@
     lax.fori_loop(0, n_groups, mix_group, 0)
     ob_s[...] = q_s[...].astype(jnp.bfloat16)
 
-    def give(t):
-        return pltpu.make_async_remote_copy(
-            src_ref=part.at[1, t], dst_ref=take_s.at[t], send_sem=give_sem.at[t], recv_sem=take_sem.at[t],
-            device_id={'side': partner}, device_id_type=MESH)
+    own_rows = pl.ds(pl.multiple_of(core * rows, rows), rows)
 
     def o_step(t, carry):
         slot = lax.rem(o_first + t, SLOTS)
         o_copy(t, slot).wait()
         y = jnp.dot(ob_s[...], ring[slot, :q_cols], preferred_element_type=jnp.float32)
-        part[1, t] = jnp.where(core == 0, y[rows:], y[:rows])
+        cols = pl.ds(pl.multiple_of(t * TILE, TILE), TILE)
+        give_ref[t] = jnp.where(core == 0, y[rows:], y[:rows])
+        own_ref[t] = jnp.where(core == 0, y[:rows], y[rows:]) + x_s[own_rows, cols].astype(jnp.float32)
+        return carry
+
+    lax.fori_loop(0, n_col, o_step, 0)
+
+
+def ffn_kernel(own_ref, give_ref, ffn_gain_ref, wg_hbm, wu_hbm, wd_hbm, out_ref, ring, take_s, x1_s, h_all, u_s, part, recv,
+               w_sem, give_sem, take_sem, h_send, h_recv, p_send, p_recv):
+    rows, width = x1_s.shape
+    depth = wd_hbm.shape[0]
+    n_col = width // TILE
+    n_ff = depth // TILE
+    per_pass = 2 * n_ff + n_col
+    n_tiles = 2 * per_pass
+
+    side = lax.axis_index('side')
+    partner = side + 1 - 2 * lax.rem(side, 2)
+    dev = lax.axis_index('dev')
+    flip = dev >= 2
+    is_end = (dev == 0) | (dev == 3)
+    is_mid = (dev == 1) | (dev == 2)
+    end_dev = jnp.where(flip, 3, 0)
+    mid_dev = jnp.where(flip, 2, 1)
+    far_dev = jnp.where(flip, 1, 2)
+
+    def column_copy(hbm, first_row, n_rows, first_col, slot):
+        cols = pl.ds(pl.multiple_of(first_col, TILE), TILE)
+        return pltpu.make_async_copy(hbm.at[pl.ds(first_row, n_rows), cols], ring.at[slot, pl.ds(0, n_rows)],
+                                     w_sem.at[slot])
+
+    def gate_copy(t, slot):
+        return column_copy(wg_hbm, 0, width, t * TILE, slot)
+
+    def up_copy(t, slot):
+        return column_copy(wu_hbm, 0, width, t * TILE, slot)
+
+    def down_copy(t, slot):
+        return column_copy(wd_hbm, 0, depth, t * TILE, slot)
+
+    def start_ff(i):
+        slot = lax.rem(i, FFN_SLOTS)
+        r = lax.rem(i, per_pass)
+        live = i < n_tiles
+
+        @pl.when(live & (r < 2 * n_ff) & (lax.rem(r, 2) == 0))
+        def _():
+            gate_copy(r // 2, slot).start()
+
+        @pl.when(live & (r < 2 * n_ff) & (lax.rem(r, 2) == 1))
+        def _():
+            up_copy(r // 2, slot).start()
+
+        @pl.when(live & (r >= 2 * n_ff))
+        def _():
+            down_copy(r - 2 * n_ff, slot).start()
+
+    def first(i, carry):
+        start_ff(i)
+        return carry
+
+    lax.fori_loop(0, FFN_SLOTS, first, 0)
+
+    def signal(target):
+        pl.semaphore_signal(pltpu.get_barrier_semaphore(), inc=1, device_id=target, device_id_type=MESH)
+
+    signal({'side': partner})
+
+    @pl.when(is_end)
+    def _():
+        signal({'dev': mid_dev})
+        pl.semaphore_wait(pltpu.get_barrier_semaphore(), 2)
+
+    @pl.when(is_mid)
+    def _():
+        signal({'dev': end_dev})
+        signal({'dev': far_dev})
+        pl.semaphore_wait(pltpu.get_barrier_semaphore(), 3)
+
+
+    def give(t):
+        return pltpu.make_async_remote_copy(
+            src_ref=give_ref.at[t], dst_ref=take_s.at[t], send_sem=give_sem.at[t], recv_sem=take_sem.at[t],
+            device_id={'side': partner}, device_id_type=MESH)
+
+    def give_step(t, carry):
         give(t).start()
-        part[0, t] = jnp.where(core == 0, y[:rows], y[rows:])
-        start_ff(ff_first - o_first + o_first + t)
-        return carry
-
-    lax.fori_loop(0, n_col, o_step, 0)
-    own_rows = pl.ds(pl.multiple_of(core * rows, rows), rows)
+        return carry
+
+    lax.fori_loop(0, n_col, give_step, 0)
 
     def x1_step(t, square):
         give(t).wait_recv()
         give(t).wait_send()
         cols = pl.ds(pl.multiple_of(t * TILE, TILE), TILE)
-        x1 = (x_s[own_rows, cols].astype(jnp.float32) + (part[0, t] + take_s[t])).astype(jnp.bfloat16)
+        x1 = (own_ref[t] + take_s[t]).astype(jnp.bfloat16)
         x1_s[:, cols] = x1
         x1_f = x1.astype(jnp.float32)
         return square + jnp.sum(x1_f * x1_f, axis=-1, keepdims=True)
@@ -314,24 +338,24 @@
 
     for half in range(2):
         def ff_step(t, carry):
-            i = ff_first + half * per_pass + 2 * t
-            slot_g, slot_u = lax.rem(i, SLOTS), lax.rem(i + 1, SLOTS)
+            i = half * per_pass + 2 * t
+            slot_g, slot_u = lax.rem(i, FFN_SLOTS), lax.rem(i + 1, FFN_SLOTS)
             h = h_all[2 * half:2 * half + 2].reshape(2 * rows, width)
             gate_copy(t, slot_g).wait()
             gate = jnp.dot(h, ring[slot_g], preferred_element_type=jnp.float32)
-            start_ff(i + SLOTS)
+            start_ff(i + FFN_SLOTS)
             up_copy(t, slot_u).wait()
             up = jnp.dot(h, ring[slot_u], preferred_element_type=jnp.float32)
-            start_ff(i + 1 + SLOTS)
+            start_ff(i + 1 + FFN_SLOTS)
             u_s[:, pl.ds(pl.multiple_of(t * TILE, TILE), TILE)] = (jax.nn.silu(gate) * up).astype(jnp.bfloat16)
             return carry
 
         def down_step(c, carry):
-            i = ff_first + half * per_pass + 2 * n_ff + c
-            slot = lax.rem(i, SLOTS)
+            i = half * per_pass + 2 * n_ff + c
+            slot = lax.rem(i, FFN_SLOTS)
             down_copy(c, slot).wait()
             y = jnp.dot(u_s[...], ring[slot, :depth], preferred_element_type=jnp.float32)
-            start_ff(i + SLOTS)
+            start_ff(i + FFN_SLOTS)
             part[2 * half, c] = y[:rows]
             part[2 * half + 1, c] = y[rows:]
 
@@ -430,28 +454,28 @@
             send_h(0, 0, k, end_dev).wait_send()
 
 
-def layer_step(hidden, lengths, k_cache, v_cache, w_q, w_kv, w_o, gain_attn, gain_ffn, w_gate, w_up, w_down, n_side):
+def attention(hidden, lengths, k_cache, v_cache, w_q, w_kv, w_o, gain, n_side):
     rows, width = hidden.shape[0] // n_side, hidden.shape[1]
     _, kv_heads, cache, head = k_cache.shape
     q_cols = w_q.shape[1] // 2
     heads = q_cols // head
-    depth = w_down.shape[0]
     n_col = width // TILE
+    keys = kv_heads // 2 * cache
     assert kv_heads * head == 2 * TILE, "tile"
     cos_tab, sin_tab = rope_tables(cache, head)
     vmem = pl.BlockSpec(memory_space=pltpu.VMEM)
     hbm = pl.BlockSpec(memory_space=pl.ANY)
     f32, bf16 = jnp.float32, jnp.bfloat16
     dma = pltpu.SemaphoreType.DMA
-    kv_block = (KV_BUFS, SEQS, kv_heads // 2, cache, head)
+    partial = jax.ShapeDtypeStruct((n_col, rows, TILE), f32)
     return pl.pallas_call(
-        functools.partial(layer_kernel, rows),
-        out_shape=jax.ShapeDtypeStruct((rows, width), bf16),
-        in_specs=[pl.BlockSpec(memory_space=pltpu.SMEM)] + [vmem] * 4 + [hbm] * 9,
-        out_specs=vmem,
+        functools.partial(attention_kernel, rows),
+        out_shape=(partial, partial),
+        in_specs=[pl.BlockSpec(memory_space=pltpu.SMEM)] + [vmem] * 3 + [hbm] * 6,
+        out_specs=(vmem, vmem),
         scratch_shapes=[
             pltpu.VMEM((SLOTS, width, TILE), bf16),
-            pltpu.VMEM(kv_block, bf16),
+            pltpu.VMEM((KV_BUFS, SEQS, kv_heads // 2, cache, head), bf16),
             pltpu.VMEM((2 * rows, width), bf16),
             pltpu.VMEM((2 * rows, width), bf16),
             pltpu.VMEM((2 * rows, head), f32),
@@ -459,20 +483,42 @@
             pltpu.VMEM((2 * rows, q_cols), f32),
             pltpu.VMEM((2 * rows, 2 * TILE), f32),
             pltpu.VMEM((2 * rows, q_cols), bf16),
-            pltpu.VMEM((2 * rows // SEQS, SEQS * heads, kv_heads // 2 * cache + head), f32),
-            pltpu.VMEM((2 * rows // SEQS, SEQS * heads, kv_heads // 2 * cache), bf16),
+            pltpu.VMEM((2 * rows // SEQS, SEQS * heads, keys + head), f32),
+            pltpu.VMEM((2 * rows // SEQS, SEQS * heads, keys), bf16),
             pltpu.VMEM((SEQS * heads, head), f32),
             pltpu.VMEM((SEQS * heads, head), f32),
             pltpu.VMEM((SEQS * heads, head), bf16),
+            dma(()),
+            dma((SLOTS,)),
+            dma((KV_BUFS,)),
+        ],
+        compiler_params=pltpu.CompilerParams(vmem_limit_bytes=VMEM_LIMIT),
+        name="attention",
+    )(lengths, jnp.asarray(cos_tab), jnp.asarray(sin_tab), gain[None], hidden, k_cache, v_cache, w_q, w_kv, w_o)
+
+
+def ffn(own, give, gain, w_gate, w_up, w_down):
+    n_col, rows, _ = own.shape
+    width = n_col * TILE
+    depth = w_down.shape[0]
+    vmem = pl.BlockSpec(memory_space=pltpu.VMEM)
+    hbm = pl.BlockSpec(memory_space=pl.ANY)
+    f32, bf16 = jnp.float32, jnp.bfloat16
+    dma = pltpu.SemaphoreType.DMA
+    return pl.pallas_call(
+        ffn_kernel,
+        out_shape=jax.ShapeDtypeStruct((rows, width), bf16),
+        in_specs=[vmem] * 3 + [hbm] * 3,
+        out_specs=vmem,
+        scratch_shapes=[
+            pltpu.VMEM((FFN_SLOTS, width, TILE), bf16),
             pltpu.VMEM((n_col, rows, TILE), f32),
             pltpu.VMEM((rows, width), bf16),
             pltpu.VMEM((4, rows, width), bf16),
             pltpu.VMEM((2 * rows, depth), bf16),
             pltpu.VMEM((4, n_col, rows, TILE), f32),
             pltpu.VMEM((5, n_col, rows, TILE), f32),
-            dma(()),
-            dma((SLOTS,)),
-            dma((KV_BUFS,)),
+            dma((FFN_SLOTS,)),
             dma((n_col,)),
             dma((n_col,)),
             dma((5,)),
@@ -481,9 +527,8 @@
             dma((5, n_col)),
         ],
         compiler_params=pltpu.CompilerParams(vmem_limit_bytes=VMEM_LIMIT, collective_id=0, has_side_effects=True),
-        name="layer",
-    )(lengths, jnp.asarray(cos_tab), jnp.asarray(sin_tab), gain_attn[None], gain_ffn[None], hidden, k_cache, v_cache,
-      w_q, w_kv, w_o, w_gate, w_up, w_down)
+        name="ffn",
+    )(own, give, gain[None], w_gate, w_up, w_down)
 
 
 def solution(mesh):
@@ -504,7 +549,7 @@
 
     def device_fn(hidden, cache_len, k_cache, v_cache, w_q, w_kv, w_o, attn_gain, ffn_gain, w_gate, w_up, w_down):
         assert w_q.shape[0] == 1, "layers"
-        return layer_step(hidden, cache_len, k_cache[0], v_cache[0], w_q[0], w_kv[0], w_o[0], attn_gain[0], ffn_gain[0],
-                          w_gate[0], w_up[0], w_down[0], n_side)
+        own, give = attention(hidden, cache_len, k_cache[0], v_cache[0], w_q[0], w_kv[0], w_o[0], attn_gain[0], n_side)
+        return ffn(own, give, ffn_gain[0], w_gate[0], w_up[0], w_down[0])
 
     return jax.shard_map(device_fn, mesh=mesh, in_specs=in_specs, out_specs=out_specs, check_vma=False)

time: 151 us -> 157 us (1.040)
  Pallas kernels: 149 us -> 155 us
    pallas_call x1 -> x2, Pallas kernels: 149 us -> 155 us  [the longest x1 113 us: ffn(): pl.pallas_call(ffn_kernel, out_shape=jax.ShapeDtypeStruct((rows, width),...]
where the time goes in v5:
time: 157 us
  Pallas kernels  155 us (99%)
  local copies, waits for them, and re-layouts  1.87 us (1%)
    pallas_call x1, Pallas kernels, ffn(): pl.pallas_call(ffn_kernel, out_shape=jax.ShapeDtypeStruct((rows, width),...  113 us
    pallas_call x1, Pallas kernels, attention(): pl.pallas_call(functools.partial(attention_kernel, rows), out_shape=(part...  41.5 us

profile of v5, /device:TPU:14, one launch (start us, length us, event | category | flops | bytes accessed | tf_op | source)
XLA Modules:
  0.0 156.7 jit_solution(3557622276008114615)
XLA Ops:
  0.0 41.5 %attention.1 = (f32[8,64,512]{2,1,0:T(8,128)}, f32[8,64,512]{2,1,0:T(8,128)}) custom-call(s32[256]{0:T(256)} %len_ref.1, f32[65,1,128]{2,1,0:T(1,128)} %constant.4.clone.cos_tab, f32[65,1,128]{2,1,0:T(1,128)} %constant.5.clone.sin_tab, f32[1,4096]{1,0:T(1,128)} %gain_ref.1, bf16[256,4096]{1,0:T(8,128)(2,1)} %x_hbm.1, bf16[256,8,64,128]{3,2,1,0:T(8,128)(2,1)} %bitcast.8, ...), custom_call_target="tpu_custom_call" | custom-call | tf_op jit(solution)/shard_map/attention/pallas_call | solution.py:471
  41.5 113.3 %ffn.1 = bf16[64,4096]{1,0:T(8,128)(2,1)} custom-call(f32[8,64,512]{2,1,0:T(8,128)} %get-tuple-element.7.own_ref, f32[8,64,512]{2,1,0:T(8,128)} %get-tuple-element.8.give_ref, f32[1,4096]{1,0:T(1,128)} %ffn_gain_ref.1, bf16[4096,3584]{1,0:T(8,128)(2,1)} %bitcast.12, bf16[4096,3584]{1,0:T(8,128)(2,1)} %bitcast.13, bf16[3584,4096]{1,0:T(8,128)(2,1)} %bitcast.14), custom_call_target="tpu_custom_call" | custom-call | tf_op jit(solution)/shard_map/ffn/pallas_call | solution.py:508
  154.8 1.9 %copy.16 = bf16[64,4096]{1,0:T(8,128)(2,1)} copy(bf16[64,4096]{1,0:T(8,128)(2,1)} %ffn.1) | data formatting | bytes 1048576

commit v6 on v4

--- a/solution.py
+++ b/solution.py
@@ -14,6 +14,7 @@
 SLOTS = 8
 SEQS = 16
 KV_BUFS = 4
+AHEAD = 3
 VMEM_LIMIT = 66_000_000
 MESH = pl.DeviceIdType.MESH
 
@@ -40,6 +41,7 @@
     group = heads // kv_heads
     pair = 2 * rows
     n_groups = pair // SEQS
+    assert n_groups == width // TILE and q_cols // TILE == AHEAD + 1, "groups"
     depth = wd_hbm.shape[0]
     n_q = q_cols // TILE
     n_col = width // TILE
@@ -121,14 +123,8 @@
 
     x_copy = pltpu.make_async_copy(x_hbm.at[pl.ds(base, pair)], x_s, x_sem)
     x_copy.start()
-    for t in range(n_q):
+    for t in range(AHEAD):
         q_copy(t, t).start()
-    for which in range(2):
-        kv_copy(which, n_q + which).start()
-    for i in range(KV_BUFS):
-        start_kv(i)
-    for t in range(SLOTS - o_first):
-        o_copy(t, o_first + t).start()
 
     def signal(target):
         pl.semaphore_signal(pltpu.get_barrier_semaphore(), inc=1, device_id=target, device_id_type=MESH)
@@ -165,10 +161,25 @@
 
     def q_step(t, carry):
         q_copy(t, t).wait()
+        ahead = t + AHEAD
+
+        @pl.when(ahead < n_q)
+        def _():
+            q_copy(ahead, ahead).start()
+
+        for which in range(2):
+            @pl.when(ahead == n_q + which)
+            def _():
+                kv_copy(which, n_q + which).start()
+
+        for i in range(KV_BUFS):
+            @pl.when(t == n_q - 1)
+            def _():
+                start_kv(i)
+
         tile = jnp.dot(a_s[...], ring[t], preferred_element_type=jnp.float32)
         for i in range(TILE // head):
             q_s[:, pl.ds(pl.multiple_of(t * TILE + i * head, head), head)] = rotated(tile, i)
-        o_copy(t + SLOTS - o_first, t).start()
         return carry
 
     lax.fori_loop(0, n_q, q_step, 0)
@@ -176,10 +187,8 @@
     tile = jnp.dot(a_s[...], ring[n_q], preferred_element_type=jnp.float32)
     for i in range(TILE // head):
         kv_s[:, i * head:(i + 1) * head] = rotated(tile, i)
-    o_copy(n_col - 2, n_q).start()
     kv_copy(1, n_q + 1).wait()
     kv_s[:, TILE:] = jnp.dot(a_s[...], ring[n_q + 1], preferred_element_type=jnp.float32)
-    o_copy(n_col - 1, n_q + 1).start()
 
     scale = head ** -0.5
     keys = kv_heads * cache
@@ -220,6 +229,8 @@
         return carry
 
     def softmax_group(g, carry):
+        o_copy(g, lax.rem(o_first + g, SLOTS)).start()
+
         def one(i, carry):
             n = len_ref[base + g * SEQS + i]
             s = jnp.where(key_pos < n, s_s[g, seq_rows(i), :keys] * scale, -1e30)

time: 151 us -> 147 us (0.974)
  Pallas kernels: 149 us -> 145 us
    pallas_call x1, Pallas kernels: 149 us -> 145 us  [layer_step(): pl.pallas_call(functools.partial(layer_kernel, rows), out_shape=jax.Shape...]
where the time goes in v6:
time: 147 us
  Pallas kernels  145 us (99%)
  local copies, waits for them, and re-layouts  1.87 us (1%)
    pallas_call x1, Pallas kernels, layer_step(): pl.pallas_call(functools.partial(layer_kernel, rows), out_shape=jax.Shape...  145 us

profile of v6, /device:TPU:14, one launch (start us, length us, event | category | flops | bytes accessed | tf_op | source)
XLA Modules:
  0.0 146.9 jit_solution(15682197993661265516)
XLA Ops:
  0.0 145.1 %layer.1 = bf16[64,4096]{1,0:T(8,128)(2,1)} custom-call(s32[256]{0:T(256)} %len_ref.1, f32[65,1,128]{2,1,0:T(1,128)} %constant.4.clone.cos_tab, f32[65,1,128]{2,1,0:T(1,128)} %constant.5.clone.sin_tab, f32[1,4096]{1,0:T(1,128)} %gain_ref.1, f32[1,4096]{1,0:T(1,128)} %ffn_gain_ref.1, bf16[256,4096]{1,0:T(8,128)(2,1)} %x_hbm.1, ...), custom_call_target="tpu_custom_call" | custom-call | tf_op jit(solution)/shard_map/layer/pallas_call | solution.py:458
  145.1 1.9 %copy.16 = bf16[64,4096]{1,0:T(8,128)(2,1)} copy(bf16[64,4096]{1,0:T(8,128)(2,1)} %layer.1) | data formatting | bytes 1048576

commit v7 on v6

--- a/solution.py
+++ b/solution.py
@@ -149,7 +149,7 @@
         sin_s[pl.ds(i, 1), :] = sin_tab[n]
         return carry
 
-    lax.fori_loop(0, pair, lookup, 0)
+    lax.fori_loop(0, pair, lookup, 0, unroll=8)
     x_copy.wait()
     x_f = x_s[...].astype(jnp.float32)
     inv = lax.rsqrt(jnp.mean(x_f * x_f, axis=-1, keepdims=True) + EPS)
@@ -279,7 +279,6 @@
         part[1, t] = jnp.where(core == 0, y[rows:], y[:rows])
         give(t).start()
         part[0, t] = jnp.where(core == 0, y[:rows], y[rows:])
-        start_ff(ff_first - o_first + o_first + t)
         return carry
 
     lax.fori_loop(0, n_col, o_step, 0)
@@ -292,6 +291,7 @@
         x1 = (x_s[own_rows, cols].astype(jnp.float32) + (part[0, t] + take_s[t])).astype(jnp.bfloat16)
         x1_s[:, cols] = x1
         x1_f = x1.astype(jnp.float32)
+        start_ff(ff_first + t)
         return square + jnp.sum(x1_f * x1_f, axis=-1, keepdims=True)
 
     square = lax.fori_loop(0, n_col, x1_step, jnp.zeros((rows, 1), jnp.float32))
@@ -351,7 +351,7 @@
                 send_part(2 * half + 1, c, 2 * half, mid_dev).start()
 
             if half == 0:
-                @pl.when(is_mid & (c == n_col - 3))
+                @pl.when(is_mid & (c == 1))
                 def _():
                     send_h(1, 3, 0, end_dev).wait_recv()
                     send_h(3, 3, 4, end_dev).start()

time: 147 us -> 145 us (0.986)
  the two profiles are of different devices: /device:TPU:14 before, /device:TPU:10 now
where the time goes in v7:
time: 145 us
  Pallas kernels  143 us (99%)
  local copies, waits for them, and re-layouts  1.87 us (1%)
    pallas_call x1, Pallas kernels, layer_step(): pl.pallas_call(functools.partial(layer_kernel, rows), out_shape=jax.Shape...  143 us

profile of v7, /device:TPU:10, one launch (start us, length us, event | category | flops | bytes accessed | tf_op | source)
XLA Modules:
  0.0 144.8 jit_solution(970289237977558500)
XLA Ops:
  0.0 142.9 %layer.1 = bf16[64,4096]{1,0:T(8,128)(2,1)} custom-call(s32[256]{0:T(256)} %len_ref.1, f32[65,1,128]{2,1,0:T(1,128)} %constant.4.clone.cos_tab, f32[65,1,128]{2,1,0:T(1,128)} %constant.5.clone.sin_tab, f32[1,4096]{1,0:T(1,128)} %gain_ref.1, f32[1,4096]{1,0:T(1,128)} %ffn_gain_ref.1, bf16[256,4096]{1,0:T(8,128)(2,1)} %x_hbm.1, ...), custom_call_target="tpu_custom_call" | custom-call | tf_op jit(solution)/shard_map/layer/pallas_call | solution.py:458
  142.9 1.9 %copy.16 = bf16[64,4096]{1,0:T(8,128)(2,1)} copy(bf16[64,4096]{1,0:T(8,128)(2,1)} %layer.1) | data formatting | bytes 1048576
